TPU v7x, 32 devices: a whole 2x2x4 slice. The times are simulated.
32 devices in a mesh: dp: 2 (over core), row: 4 (over y, x), col: 4 (over z).
Axes of the slice: x: 2, y: 2, z: 4, core: 2. Of those that a mesh axis runs over, the one named last changes fastest.
Arguments:
- states: bfloat16 [3072, 4096], P(('dp', 'row'), 'col'), may hold values from -6 to 6
- actions: bfloat16 [3072, 24], P(('dp', 'row')), may hold values from -6 to 6
- rewards: float32 [3072], P(('dp', 'row')), may hold values from -6 to 6
- terminal: int32 [3072], P(('dp', 'row')), may hold values 0 or 1
- next_index: int32 [3072], P(('dp', 'row')), may hold values from 0 to 3071
- hidden_weights: bfloat16 [4, 4096, 4096], P(None, 'col', 'row'), may hold values from -0.09375 to 0.09375
- action_weights: bfloat16 [2, 24, 4096], replicated, may hold values from -1.25 to 1.25
- heads: bfloat16 [4096, 27], replicated, may hold values from -0.09375 to 0.09375
- policy_scale: float32 [24], replicated, may hold values from 0.5 to 2
Outputs:
- advantage: float32 [3072], P(('dp', 'row'))
- losses: float32 [3], replicated
- head_grads: float32 [4096, 27], replicated
Inputs may be any that keep to these rules, and one draw needn't show every extreme that they name: `next_index`: any batch row, from any device.
All inputs are finite; a program needn't handle non-finite values. No bound on the sum of `terminal` on one device may be relied on, other than what follows from the above.
Results may differ from a plain program's by a relative error of at most 0.0038.
Values may be sent and summed in bfloat16 or wider, within the bound.
No kernel may reach another device: no remote copies, remote signals or barrier semaphores. Data moves between devices by JAX's collectives and lax.ppermute only.
A program may use at most 128 MiB of HBM per device.

v0:
```python
import math

import jax
import jax.numpy as jnp
from jax import lax
from jax.sharding import PartitionSpec as P

D = 4096


GAMMA = 0.99
TAU = 0.7
FLOOR = 0.01


def head_parts(hidden, head_rows):
    first_part = jnp.dot(hidden[0], head_rows[:, 0], preferred_element_type=jnp.float32)
    second_part = jnp.dot(hidden[1], head_rows[:, 1], preferred_element_type=jnp.float32)
    value_part = jnp.dot(hidden[2], head_rows[:, 2], preferred_element_type=jnp.float32)
    mean_part = jnp.dot(hidden[3], head_rows[:, 3:], preferred_element_type=jnp.float32)
    return (first_part, second_part, value_part, mean_part)


def shards(
    states,
    actions,
    rewards,
    terminal,
    next_index,
    hidden_weights,
    action_weights,
    heads,
    policy_scale,
):
    rows_here = states.shape[0]
    row_count = lax.axis_size("row")
    col_count = lax.axis_size("col")
    col_at = lax.axis_index("col")
    row_at = lax.axis_index("row")
    col_units = D // col_count
    row_units = D // row_count
    tile_units = D // (row_count * col_count)
    total_rows = rows_here * lax.axis_size("dp") * row_count
    all_states, all_actions = (
        lax.all_gather(states, "row", axis=0, tiled=True),
        lax.all_gather(actions, "row", axis=0, tiled=True),
    )
    terms = jnp.einsum(
        "bk,nko->nbo", all_states, hidden_weights, preferred_element_type=jnp.float32
    )
    summed = lax.psum_scatter(terms, "col", scatter_dimension=2, tiled=True)
    act_cols = lax.dynamic_slice_in_dim(
        action_weights, row_at * row_units + col_at * tile_units, tile_units, 2
    )
    extra = jnp.einsum("ba,nau->nbu", all_actions, act_cols, preferred_element_type=jnp.float32)
    pre = jnp.concatenate([summed[:2] + extra, summed[2:]], axis=0)
    local_hidden = jnp.maximum(pre, 0.0).astype(jnp.bfloat16)
    hidden = lax.all_to_all(local_hidden, "row", split_axis=1, concat_axis=2, tiled=True)
    blocks = heads.reshape(row_count, col_count, tile_units, heads.shape[1])
    head_rows = lax.dynamic_index_in_dim(blocks, col_at, 1, keepdims=False).reshape(
        col_units, heads.shape[1]
    )
    parts = head_parts(hidden, head_rows)
    first_q, second_q, value, policy_mean = lax.psum(
        (parts[0], parts[1], parts[2], parts[3]), "col"
    )
    advantage = jnp.minimum(first_q, second_q) - value
    value_whole = lax.all_gather(value, ("dp", "row"), axis=0, tiled=True)
    top = lax.pmax(jnp.max(advantage), ("dp", "row"))
    target = rewards + GAMMA * (1.0 - terminal.astype(jnp.float32)) * jnp.take(
        value_whole, next_index, axis=0
    )
    weight = jnp.maximum(jnp.exp(advantage - top), FLOOR)
    expectile = jnp.where(advantage >= 0.0, TAU, 1.0 - TAU)
    scaled = (actions.astype(jnp.float32) - policy_mean) / policy_scale
    log_prob = -0.5 * jnp.sum(scaled * scaled, axis=1)
    value_terms = expectile * advantage * advantage
    critic_terms = (first_q - target) ** 2 + (second_q - target) ** 2
    policy_terms = -weight * log_prob
    coeff_first = (2.0 * (first_q - target))[:, None]
    coeff_second = (2.0 * (second_q - target))[:, None]
    coeff_value = (-2.0 * expectile * advantage)[:, None]
    coeff_policy = -weight[:, None] * scaled / policy_scale
    loss_terms = jnp.stack([jnp.sum(value_terms), jnp.sum(critic_terms), jnp.sum(policy_terms)])
    columns = [
        (hidden[0], coeff_first),
        (hidden[1], coeff_second),
        (hidden[2], coeff_value),
        (hidden[3], coeff_policy),
    ]
    grad_local = jnp.concatenate(
        [
            jnp.dot(units.astype(jnp.float32).T, coeff, precision=lax.Precision.HIGHEST)
            for units, coeff in columns
        ],
        axis=1,
    )
    grad_sum, loss_sum = lax.psum((grad_local, loss_terms), ("dp", "row"))
    grad_whole = lax.all_gather(grad_sum, "col", axis=0, tiled=True)
    grad_whole = (
        grad_whole.reshape(col_count, row_count, tile_units, grad_whole.shape[1])
        .transpose(1, 0, 2, 3)
        .reshape(D, grad_whole.shape[1])
    )
    return (advantage, loss_sum / total_rows, grad_whole / math.sqrt(total_rows))


def solution(mesh):
    return jax.shard_map(
        shards,
        mesh=mesh,
        in_specs=(
            P(("dp", "row"), "col"),
            P(("dp", "row"), None),
            P(("dp", "row")),
            P(("dp", "row")),
            P(("dp", "row")),
            P(None, "col", "row"),
            P(),
            P(),
            P(),
        ),
        out_specs=(P(("dp", "row")), P(), P()),
        check_vma=False,
    )
```

profile of v0, /device:TPU:0, one launch (start us, length us, event | category | flops | bytes accessed | tf_op | source)
XLA Modules:
  0.0 712.9 jit_solution(5146558858824065807)
XLA Ops:
  8.0 48.5 %all-gather.3.cloned.1.call-done = bf16[1536,1024]{1,0:T(8,128)(2,1)} async-done(((bf16[384,1024]{1,0:T(8,128)(2,1)}), bf16[1536,1024]{1,0:T(8,128)(2,1)}) %all-gather.3.cloned.1.call-update) | async-done | bytes 3145744 | tf_op jit(solution)/shard_map/all_gather | solution.py:45
  56.4 21.2 %convolution_bitcast_fusion = f32[4,1536,1024]{1,2,0:T(8,128)} fusion(bf16[4,1024,1024]{2,1,0:T(8,128)(2,1)} %param.14, bf16[1536,1024]{1,0:T(8,128)(2,1)} %all-gather.3.cloned.1.call-done), kind=kOutput, calls=%fused_computation.1 | convolution fusion | flops 12884901888 | bytes 36700160 | tf_op jit(solution)/shard_map/bk,nko->nbo/dot_general | solution.py:48
  78.3 8.3 %all_gather.13 = bf16[1536,24]{0,1:T(8,128)(2,1)S(1)} all-gather(bf16[384,24]{0,1:T(8,128)(2,1)S(1)} %copy-done.1), channel_id=1, replica_groups=mesh['dp'=2,'row'=4,'col'=4] {'row'}, dimensions={0}, use_global_device_ids=true | all-gather | bytes 92160 | tf_op jit(solution)/shard_map/all_gather | solution.py:46
  86.7 405.3 %reduce-scatter.2.cloned.1.call-done = f32[4,1536,256]{1,2,0:T(8,128)} async-done(((f32[4,1536,1024]{1,2,0:T(8,128)}), f32[4,1536,256]{1,2,0:T(8,128)}) %reduce-scatter.2.cloned.1.call-update) | async-done | bytes 6291472 | tf_op jit(solution)/shard_map/reduce_scatter | solution.py:51
  492.0 2.1 slice.51
  494.1 2.5 fusion.1
  497.2 3.6 copy.23
  500.8 3.8 all-to-all-start
  504.7 1.7 reshape.44
  506.5 1.3 dynamic-slice_reduce_fusion
  508.5 32.6 %all-to-all-done = bf16[4,1536,256]{2,0,1:T(4,128)(2,1)S(1)} async-done(((bf16[4,1536,256]{2,0,1:T(4,128)(2,1)}), bf16[4,1536,256]{2,0,1:T(4,128)(2,1)S(1)}, u32[]{:S(2)}, u32[]{:S(2)}) %all-to-all-start) | async-done | bytes 3145760 | tf_op jit(solution)/shard_map/all_to_all | solution.py:58
  541.5 1.1 fusion.18
  543.3 0.9 convolution_reduce_fusion
  544.3 0.9 convolution_reduce_fusion.2
  545.6 0.9 convolution_reduce_fusion.1
  546.5 1.5 copy.29
  548.0 1.7 fusion.4
  549.7 21.4 %all-reduce = (f32[384]{0:T(512)}, f32[384]{0:T(512)}, f32[384]{0:T(512)}, f32[384,24]{0,1:T(8,128)}) all-reduce(f32[384]{0:T(512)S(1)} %convolution_reduce_fusion, f32[384]{0:T(512)S(1)} %convolution_reduce_fusion.2, f32[384]{0:T(512)S(1)} %convolution_reduce_fusion.1, ...), channel_id=1, replica_groups=mesh['dp'=2,'row'=4,'col'=4] {'col'}, use_global_device_ids=true, to_apply=%region_3.4 | all-reduce | flops 10368 | bytes 82944 | tf_op jit(solution)/shard_map/psum | solution.py:64
  571.8 18.9 %all-gather = f32[8,1,384]{2,1,0:T(1,128)S(1)} all-gather(f32[1,1,384]{2,1,0:T(1,128)S(1)} %reshape.55), channel_id=1, replica_groups=mesh['dp'=2,'row'=4,'col'=4] {'dp','row'}, dimensions={0}, use_global_device_ids=true | all-gather | bytes 13824 | tf_op jit(solution)/shard_map/all_gather | solution.py:68
  590.7 3.7 gather_fusion
  594.4 0.7 broadcast_multiply_fusion.2
  595.1 1.9 broadcast_multiply_fusion.1
  597.6 15.1 %pmax.7 = f32[]{:T(128)} all-reduce(f32[]{:T(128)} %get-tuple-element.4), channel_id=1, replica_groups=mesh['dp'=2,'row'=4,'col'=4] {'dp','row'}, use_global_device_ids=true, to_apply=%region_7.8 | all-reduce | flops 1 | bytes 8 | tf_op jit(solution)/shard_map/pmax | solution.py:69
  612.7 0.9 multiply_reduce_fusion
  613.5 1.3 multiply_reduce_fusion.1
  614.8 2.5 pad_maximum_fusion.1
  617.3 15.5 %psum.46 = f32[3]{0:T(128)} all-reduce(f32[3]{0:T(128)} %pad_maximum_fusion.1), channel_id=1, replica_groups=mesh['dp'=2,'row'=4,'col'=4] {'dp','row'}, use_global_device_ids=true, to_apply=%region_11.12 | all-reduce | flops 3 | bytes 24 | tf_op jit(solution)/shard_map/psum | solution.py:98
  632.7 1.5 fusion.6
  637.8 1.2 broadcast_multiply_fusion.3
  639.0 50.8 %all-reduce.3.cloned.1.call-done = f32[1024,27]{0,1:T(8,128)} async-done(((f32[1024,27]{0,1:T(8,128)}), f32[1024,27]{0,1:T(8,128)}) %all-reduce.3.cloned.1.call-update) | async-done | bytes 110608 | tf_op jit(solution)/shard_map/psum | solution.py:98
  689.8 15.1 %all_gather.15 = f32[4096,27]{0,1:T(8,128)S(1)} all-gather(f32[1024,27]{0,1:T(8,128)} %all-reduce.3.cloned.1.call-done), channel_id=1, replica_groups=mesh['dp'=2,'row'=4,'col'=4] {'col'}, dimensions={0}, use_global_device_ids=true | all-gather | bytes 552960 | tf_op jit(solution)/shard_map/all_gather | solution.py:99
  705.4 1.0 div.37
  (35 shorter events, 9.6 us)
Async XLA Ops:
  7.2 486.9 %copy-start = (bf16[2,24,4096]{2,1,0:T(8,128)(2,1)S(1)}, bf16[2,24,4096]{2,1,0:T(8,128)(2,1)}, u32[]{:S(2)}) copy-start(bf16[2,24,4096]{2,1,0:T(8,128)(2,1)} %param.15) | copy-start | bytes 1179652
  7.2 49.3 %all-gather.3.cloned.1.call-start = ((), (), s32[]{:S(2)}) async-start(), calls=%async_computation.2 | async-start | bytes 3932160 | tf_op jit(solution)/shard_map/all_gather | solution.py:45
  7.9 484.1 %reduce-scatter.2.cloned.1.call-start = ((), (), s32[]{:S(2)}) async-start(), calls=%async_computation.3 | async-start | bytes 31457280 | tf_op jit(solution)/shard_map/reduce_scatter | solution.py:51
  77.6 0.7 copy-start.1
  500.8 7.6 %copy-start.3 = (s32[384]{0:T(512)S(1)}, s32[384]{0:T(512)}, u32[]{:S(2)}) copy-start(s32[384]{0:T(512)} %param.13) | copy-start | bytes 4612
  500.8 40.2 %all-to-all-start = ((bf16[4,1536,256]{2,0,1:T(4,128)(2,1)}), bf16[4,1536,256]{2,0,1:T(4,128)(2,1)S(1)}, u32[]{:S(2)}, u32[]{:S(2)}) async-start(bf16[4,1536,256]{2,0,1:T(4,128)(2,1)} %copy.23), calls=%async_computation.1 | async-start | bytes 6291456 | tf_op jit(solution)/shard_map/all_to_all | solution.py:58
  504.7 185.1 %all-reduce.3.cloned.1.call-start = ((), (), s32[]{:S(2)}) async-start(), calls=%async_computation.4 | async-start | bytes 262144 | tf_op jit(solution)/shard_map/psum | solution.py:98
  597.0 108.3 %copy-start.2 = (f32[384]{0:T(512)}, f32[384]{0:T(512)S(1)}, u32[]{:S(2)}) copy-start(f32[384]{0:T(512)S(1)} %get-tuple-element.22) | copy-start | bytes 4612
Sparse Core Ops, SparseCore 0:
  9.8 46.5 all-gather.2
  77.8 414.1 reduce-scatter.1
  638.0 51.7 all-reduce.2
where the time goes:
time: 714 us; the launch traced here: 713 us
  waiting for transfers between devices  538 us (75%)
  blocking collectives  94.3 us (13%)
  matrix products  31.8 us (4%)
  local copies, waits for them, and re-layouts  20.7 us (3%)
  between operations  13.9 us (2%)
  other arithmetic  10.4 us (1%)
    reduce_scatter x1, waiting for transfers between devices, shards(): summed = lax.psum_scatter(terms, 'col', scatter_dimension=2, tiled=True)  405 us
    psum x1, waiting for transfers between devices, shards(): grad_sum, loss_sum = lax.psum((grad_local, loss_terms), ('dp', 'row'))  50.8 us
    all_gather x1, waiting for transfers between devices, shards(): lax.all_gather(states, 'row', axis=0, tiled=True)  48.5 us
    all_to_all x1, waiting for transfers between devices, shards(): lax.all_to_all(local_hidden, 'row', split_axis=1, concat_axis=2, tiled=True)  32.6 us
    psum x1, blocking collectives, shards(): lax.psum((parts[0], parts[1], parts[2], parts[3]), 'col')  21.4 us
    dot_general x1, matrix products, shards(): jnp.einsum('bk,nko->nbo', all_states, hidden_weights, preferred_element_t...  21.2 us
    all_gather x1, blocking collectives, shards(): value_whole = lax.all_gather(value, ('dp', 'row'), axis=0, tiled=True)  18.9 us
    psum x1, blocking collectives, shards(): grad_sum, loss_sum = lax.psum((grad_local, loss_terms), ('dp', 'row'))  15.5 us
  transfers between devices with their start and end apart: 4, of which 4 were waited for; matrix products, arithmetic and copies ran while one was open for 1% of the time, Pallas kernels for 0%

commit v1 on v0

v1 whole, which is shorter than its diff:
```python
import functools
import math

import jax
import jax.numpy as jnp
from jax import lax
from jax.experimental import pallas as pl
from jax.experimental.pallas import tpu as pltpu
from jax.sharding import PartitionSpec as P


GAMMA = 0.99
TAU = 0.7
FLOOR = 0.01
ORDER = (3, 2, 0, 1)
F32 = jnp.float32
BF16 = jnp.bfloat16


def swap(x, axis, bit):
    size = lax.axis_size(axis)
    return lax.ppermute(x, axis, [(i, i ^ bit) for i in range(size)])


def spread(x, axes):
    size = math.prod(lax.axis_size(a) for a in axes)
    x = jnp.broadcast_to(x[None], (size,) + x.shape)
    return lax.all_to_all(x, axes, 0, 0, tiled=True)


def bits_of(size):
    return [1 << b for b in range(size.bit_length() - 1)]


def net_kernel(row_ref, *refs, places, row_count, nets, with_actions):
    count = len(places)
    pieces = refs[:count]
    own_ref, other_ref = refs[count : count + 2]
    at = count + 2
    head_refs = refs[at : at + nets]
    at += nets
    if with_actions:
        act_ref, act_w_ref = refs[at : at + 2]
        at += 2
    hidden_refs = refs[at : at + nets]
    part_refs = refs[at + nets : at + 2 * nets]
    buf, w_buf, sems, w_sems = refs[at + 2 * nets :]
    w_copies = [
        pltpu.make_async_copy(ref, w_buf.at[i], w_sems.at[i])
        for i, ref in enumerate((own_ref, other_ref))
    ]
    copies = [
        pltpu.make_async_copy(pieces[i], buf.at[j, :, pl.ds(start, size), :], sems.at[i])
        for i, (j, start, size) in enumerate(places)
    ]
    row = row_ref[0]
    w_copies[0].start()
    for j in range(row_count):
        for i, (jj, _, _) in enumerate(places):
            if jj == j:
                copies[i].start()
        if j == 0:
            w_copies[1].start()
    for w_copy in w_copies:
        w_copy.wait()
    for j in range(row_count):
        for i, (jj, _, _) in enumerate(places):
            if jj == j:
                copies[i].wait()
        where = jnp.bitwise_xor(row, j)
        for n in range(nets):
            acc = jnp.dot(buf[j, 0], w_buf[0, n], preferred_element_type=F32)
            acc = acc + jnp.dot(buf[j, 1], w_buf[1, n], preferred_element_type=F32)
            if with_actions:
                acc = acc + jnp.dot(act_ref[where], act_w_ref[n], preferred_element_type=F32)
            hidden = jnp.maximum(acc, 0.0).astype(BF16)
            hidden_refs[n][where] = hidden
    for n in range(nets):
        for j in range(row_count):
            part_refs[n][j] = lax.dot_general(
                head_refs[n][...], hidden_refs[n][j], (((1,), (1,)), ((), ())),
                preferred_element_type=F32,
            )


def run_nets(row_at, pieces, places, w_own, w_other, heads, rows, row_count, extra):
    nets, depth, units = w_own.shape
    any_spec = pl.BlockSpec(memory_space=pl.ANY)
    vmem = pl.BlockSpec(memory_space=pltpu.VMEM)
    smem = pl.BlockSpec(memory_space=pltpu.SMEM)
    late = [w_own, w_other, *heads, *extra]
    tokens = row_count * rows
    wide = max(units, 128)
    held = 4 * tokens * depth + 8 * nets * depth * wide + 4 * nets * tokens * wide
    outs = pl.pallas_call(
        functools.partial(
            net_kernel, places=places, row_count=row_count, nets=nets,
            with_actions=bool(extra),
        ),
        out_shape=tuple(
            [jax.ShapeDtypeStruct((row_count, rows, units), BF16)] * nets
            + [jax.ShapeDtypeStruct((row_count, h.shape[0], rows), F32) for h in heads]
        ),
        in_specs=[smem] + [any_spec] * (len(pieces) + 2) + [vmem] * (len(late) - 2),
        out_specs=tuple([vmem] * (2 * nets)),
        scratch_shapes=[
            pltpu.VMEM((row_count, 2, rows, depth), BF16),
            pltpu.VMEM((2, nets, depth, units), BF16),
            pltpu.SemaphoreType.DMA((len(pieces),)),
            pltpu.SemaphoreType.DMA((2,)),
        ],
        compiler_params=pltpu.CompilerParams(vmem_limit_bytes=held + 4 * 1024 * 1024),
        cost_estimate=pl.CostEstimate(
            flops=4 * nets * tokens * depth * units,
            bytes_accessed=4 * tokens * depth,
            transcendentals=0,
        ),
    )(row_at.reshape(1), *pieces, *late)
    return outs[:nets], outs[nets:]


def split_dot(coeff, hidden):
    high = coeff.astype(BF16)
    low = (coeff - high.astype(F32)).astype(BF16)
    out = jnp.dot(high, hidden, preferred_element_type=F32)
    return out + jnp.dot(low, hidden, preferred_element_type=F32)


def tail_kernel(
    dp_ref, late_ref, pack_ref, known_ref, scale_ref, h0, h1, h2, h3,
    adv_ref, out_ref, grad_ref, *, acts,
):
    tokens = late_ref.shape[-1]
    dp = dp_ref[0]
    values = [known_ref[acts + d : acts + d + 1] for d in range(2)]
    advs = [
        jnp.minimum(late_ref[2 * d : 2 * d + 1], late_ref[2 * d + 1 : 2 * d + 2]) - values[d]
        for d in range(2)
    ]
    first, second, adv = late_ref[0:1], late_ref[1:2], advs[0]
    top = functools.reduce(jnp.maximum, [jnp.max(a) for a in advs])
    values = [jnp.where(dp == 0, values[0], values[1]), jnp.where(dp == 0, values[1], values[0])]
    rewards = pack_ref[acts : acts + 1]
    terminal = pack_ref[acts + 1 : acts + 2]
    index = pack_ref[acts + 2 : acts + 3].astype(jnp.int32)
    lanes = 128
    groups = tokens // lanes
    table = jnp.concatenate(
        [v[:, g * lanes : (g + 1) * lanes] for v in values for g in range(groups)], axis=0
    )
    high = jnp.right_shift(index, 7)
    low = jnp.bitwise_and(index, lanes - 1)
    pick_high = (lax.broadcasted_iota(jnp.int32, (table.shape[0], tokens), 0) == high).astype(F32)
    rows = lax.dot_general(
        table, pick_high, (((0,), (0,)), ((), ())), precision=lax.Precision.HIGHEST,
        preferred_element_type=F32,
    )
    pick_low = lax.broadcasted_iota(jnp.int32, (lanes, tokens), 0) == low
    following = jnp.sum(jnp.where(pick_low, rows, 0.0), axis=0, keepdims=True)
    target = rewards + GAMMA * (1.0 - terminal) * following
    weight = jnp.maximum(jnp.exp(adv - top), FLOOR)
    expectile = jnp.where(adv >= 0.0, TAU, 1.0 - TAU)
    scale = scale_ref[...]
    scaled = (pack_ref[0:acts] - known_ref[0:acts]) / scale
    log_prob = -0.5 * jnp.sum(scaled * scaled, axis=0, keepdims=True)
    gap0 = first - target
    gap1 = second - target
    loss0 = jnp.sum(expectile * adv * adv)
    loss1 = jnp.sum(gap0 * gap0 + gap1 * gap1)
    loss2 = -jnp.sum(weight * log_prob)
    adv_ref[...] = adv
    lane = lax.broadcasted_iota(jnp.int32, (1, grad_ref.shape[1]), 1)
    loss = jnp.where(lane == 0, loss0, jnp.where(lane == 1, loss1, jnp.where(lane == 2, loss2, 0.0)))
    high = loss.astype(BF16).astype(F32)
    grad_ref[acts + 3 : acts + 4] = high
    grad_ref[acts + 4 : acts + 5] = loss - high
    grad_ref[0:1] = split_dot(2.0 * gap0, h0[...])
    grad_ref[1:2] = split_dot(2.0 * gap1, h1[...])
    grad_ref[2:3] = split_dot(-2.0 * expectile * adv, h2[...])
    grad_ref[3 : 3 + acts] = split_dot(-weight * scaled / scale, h3[...])
    out = grad_ref[...].astype(BF16)
    for i in range(out_ref.shape[0]):
        out_ref[i] = out


def shards(
    states, actions, rewards, terminal, next_index, hidden_weights, action_weights, heads, policy_scale
):
    rows, feats = states.shape
    acts = actions.shape[1]
    nets, _, row_units = hidden_weights.shape
    row_count = lax.axis_size("row")
    col_count = lax.axis_size("col")
    dp_count = lax.axis_size("dp")
    dp_at = lax.axis_index("dp")
    row_at = lax.axis_index("row")
    col_at = lax.axis_index("col")
    peers = row_count * col_count
    units = row_units // col_count
    half = feats // 2
    tokens = rows * row_count
    total = tokens * dp_count
    shares = (1, 2, 3, 3, 3) if rows % 192 == 0 else (1,)
    sizes = [rows * s // sum(shares) for s in shares]
    starts = [sum(sizes[:c]) for c in range(len(sizes))]

    pack = jnp.concatenate(
        [
            actions.astype(F32).T,
            rewards[None],
            terminal.astype(F32)[None],
            next_index.astype(F32)[None],
        ],
        axis=0,
    )
    pack = spread(pack, ("row",))
    own_actions = pack[:, :acts].transpose(0, 2, 1).astype(BF16)
    pack = pack.transpose(1, 0, 2).reshape(acts + 3, tokens)

    col_bits = bits_of(col_count)[::-1]
    cols = [0]
    for bit in col_bits:
        cols = cols + [c ^ bit for c in cols]
    pair = states.reshape(rows, 2, half).transpose(1, 0, 2)
    pair = jnp.where(dp_at == 0, pair, pair[::-1])
    pieces, places = [], []
    for c, (start, size) in enumerate(zip(starts, sizes)):
        block = pair[:, start : start + size]
        for bit in col_bits:
            block = jnp.concatenate([block, swap(block, "col", bit)], axis=2)
        held = {0: block}
        order = bits_of(row_count)
        if c % 2:
            order = order[::-1]
        for bit in order:
            for j, value in list(held.items()):
                held[j ^ bit] = swap(value, "row", bit)
        for j in range(row_count):
            pieces.append(held[j])
            places.append((j, start, size))

    hidden, parts = {}, {}
    unit_at = row_at * row_units + col_at * units
    heads_t = lax.dynamic_slice_in_dim(heads.T, unit_at, units, 1)
    act_w = lax.dynamic_slice_in_dim(action_weights, unit_at, units, 2)
    for first in range(0, nets, 2):
        group = ORDER[first : first + 2]
        low = min(group)
        mine = lax.dynamic_slice(
            hidden_weights, (low, dp_at * half, 0), (len(group), half, row_units)
        )
        got = []
        for k in cols:
            sent = lax.dynamic_slice_in_dim(mine, jnp.bitwise_xor(col_at, k) * units, units, 2)
            got.append(swap(sent, "col", k) if k else sent)
        w_own = jnp.concatenate(got, axis=1)
        w_other = swap(w_own, "dp", 1)
        group = range(low, low + len(group))
        head = [
            heads_t[3:] if n == 3 else jnp.pad(heads_t[n : n + 1], ((0, 7), (0, 0))) for n in group
        ]
        extra = (own_actions, act_w) if low == 0 else ()
        got_hidden, got_parts = run_nets(
            row_at, pieces, places, w_own, w_other, head, rows, row_count, extra
        )
        for i, n in enumerate(group):
            hidden[n], parts[n] = got_hidden[i].reshape(tokens, units), got_parts[i]

    piece = tokens // peers
    known = jnp.concatenate([parts[3], parts[2][:, :1]], axis=1)
    known = known.transpose(1, 0, 2).reshape(acts + 1, peers, piece).transpose(1, 0, 2)
    known = lax.all_to_all(known, ("row", "col"), 0, 0, tiled=True)
    known = jnp.sum(known, axis=0)
    known = jnp.concatenate([known, swap(known[acts:], "dp", 1)], axis=0)
    known = spread(known, ("row", "col"))
    known = known.transpose(1, 0, 2).reshape(acts + 2, tokens)

    late = jnp.concatenate([parts[n][:, 0].reshape(1, tokens) for n in (0, 1)], axis=0)
    for axis, size in (("col", col_count), ("row", row_count)):
        late = sum((swap(late, axis, k) for k in range(1, size)), late)
    late = jnp.concatenate([late, swap(late, "dp", 1)], axis=0)

    vmem = pl.BlockSpec(memory_space=pltpu.VMEM)
    smem = pl.BlockSpec(memory_space=pltpu.SMEM)
    adv, last = pl.pallas_call(
        functools.partial(tail_kernel, acts=acts),
        out_shape=(
            jax.ShapeDtypeStruct((1, tokens), F32),
            jax.ShapeDtypeStruct((dp_count * peers, acts + 5, units), BF16),
        ),
        in_specs=[smem] + [vmem] * 8,
        out_specs=(vmem, vmem),
        scratch_shapes=[pltpu.VMEM((acts + 5, units), F32)],
        compiler_params=pltpu.CompilerParams(vmem_limit_bytes=24 * 1024 * 1024),
    )(
        dp_at.reshape(1), late, pack, known, policy_scale[:, None],
        hidden[0], hidden[1], hidden[2], hidden[3],
    )
    advantage = lax.dynamic_slice_in_dim(adv[0], row_at * rows, rows, 0)
    last = lax.all_to_all(last, ("dp", "row", "col"), 0, 0, tiled=True)
    last = last.reshape(dp_count, peers, acts + 5, units)
    summed = jnp.sum(last.astype(F32), axis=0)
    grads = summed[:, : acts + 3].transpose(1, 0, 2).reshape(acts + 3, peers * units)
    grads = (grads / math.sqrt(total)).T
    losses = (summed[0, acts + 3, :3] + summed[0, acts + 4, :3]) / total
    return advantage, losses, grads


def solution(mesh):
    return jax.shard_map(
        shards,
        mesh=mesh,
        in_specs=(
            P(("dp", "row"), "col"),
            P(("dp", "row"), None),
            P(("dp", "row")),
            P(("dp", "row")),
            P(("dp", "row")),
            P(None, "col", "row"),
            P(),
            P(),
            P(),
        ),
        out_specs=(P(("dp", "row")), P(), P()),
        check_vma=False,
    )
```

time: 714 us -> 359 us (0.50)
  waiting for transfers between devices: 538 us -> 197 us
  blocking collectives: 94.3 us -> 0 us
  starting transfers between devices: 3.95 us -> 70.3 us
  local copies, waits for them, and re-layouts: 20.7 us -> 62.6 us
  matrix products: 31.8 us -> 0 us
  Pallas kernels: 0 us -> 22.2 us
  between operations: 13.9 us -> 1.31 us
    reduce_scatter x1 -> x0, waiting for transfers between devices: 405 us -> none  [shards(): summed = lax.psum_scatter(terms, 'col', scatter_dimension=2, tiled=True)]
    ppermute x0 -> x41, waiting for transfers between devices: none -> 155 us  [swap(): return lax.ppermute(x, axis, [(i, i ^ bit) for i in range(size)])]
    ppermute x0 -> x41, starting transfers between devices: none -> 55.2 us  [swap(): return lax.ppermute(x, axis, [(i, i ^ bit) for i in range(size)])]
    psum x1 -> x0, waiting for transfers between devices: 50.8 us -> none  [shards(): grad_sum, loss_sum = lax.psum((grad_local, loss_terms), ('dp', 'row'))]
    all_gather x1 -> x0, waiting for transfers between devices: 48.5 us -> none  [shards(): lax.all_gather(states, 'row', axis=0, tiled=True)]
    all_gather x3 -> x0, blocking collectives: 42.4 us -> none  [the longest x1 18.9 us: shards(): value_whole = lax.all_gather(value, ('dp', 'row'), axis=0, tiled=True)]
    unnamed x11 -> x118, local copies, waits for them, and re-layouts: 2.05 us -> 43.6 us
    psum x2 -> x0, blocking collectives: 36.9 us -> none  [the longest x1 21.4 us: shards(): lax.psum((parts[0], parts[1], parts[2], parts[3]), 'col')]
  transfers between devices with their start and end apart: 4 -> 45, of which waited for: 4 -> 23; matrix products, arithmetic and copies ran while one was open for 1% -> 7% of each run, Pallas kernels for 0% -> 6%
where the time goes in v1:
time: 359 us; the launch traced here: 358 us
  waiting for transfers between devices  197 us (55%)
  starting transfers between devices  70.3 us (20%)
  local copies, waits for them, and re-layouts  62.6 us (17%)
  Pallas kernels  22.2 us (6%)
  other arithmetic  3.99 us (1%)
    ppermute x41, waiting for transfers between devices, swap(): return lax.ppermute(x, axis, [(i, i ^ bit) for i in range(size)])  155 us
    ppermute x41, starting transfers between devices, swap(): return lax.ppermute(x, axis, [(i, i ^ bit) for i in range(size)])  55.2 us
    unnamed x118, local copies, waits for them, and re-layouts  43.6 us
    all_to_all x2, waiting for transfers between devices, spread(): return lax.all_to_all(x, axes, 0, 0, tiled=True)  25.9 us
    pallas_call x2, Pallas kernels, run_nets(): pl.pallas_call(functools.partial(net_kernel, places=places, row_count=row...  20.5 us
    all_to_all x1, waiting for transfers between devices, shards(): last = lax.all_to_all(last, ('dp', 'row', 'col'), 0, 0, tiled=True)  15.7 us
    all_to_all x2, starting transfers between devices, spread(): return lax.all_to_all(x, axes, 0, 0, tiled=True)  7.92 us
  transfers between devices with their start and end apart: 45, of which 23 were waited for; matrix products, arithmetic and copies ran while one was open for 7% of the time, Pallas kernels for 6%

profile of v1, /device:TPU:0, one launch (start us, length us, event | category | flops | bytes accessed | tf_op | source)
XLA Modules:
  0.0 357.5 jit_solution(3923868476337178411)
XLA Ops:
  2.7 4.1 %collective-permute-start = (bf16[2,32,512]{2,1,0:T(8,128)(2,1)S(1)}, bf16[2,32,512]{2,1,0:T(8,128)(2,1)S(1)}, u32[]{:S(2)}, u32[]{:S(2)}) collective-permute-start(bf16[2,32,512]{2,1,0:T(8,128)(2,1)S(1)} %slice.70), channel_id=1, source_target_pairs={{0,2},{1,3},{2,0},{3,1},{4,6},{5,7},{6,4},{7,5},{8,10},{9,11},{10,... | collective-permute-start | bytes 196616 | tf_op jit(solution)/shard_map/ppermute | solution.py:22
  6.8 6.7 %constant_dynamic-slice_fusion.9 = (bf16[2,512,256]{2,1,0:T(8,128)(2,1)S(1)}, bf16[2,512,256]{2,1,0:T(8,128)(2,1)S(1)}, bf16[2,512,256]{2,1,0:T(8,128)(2,1)S(1)}...) fusion(bf16[4,1024,1024]{2,1,0:T(8,128)(2,1)} %param.14, ...), kind=kLoop, calls=%fused_computation.37 | loop fusion | bytes 8388628 | tf_op jit(solution)/shard_map/dynamic_slice | solution.py:254
  13.6 2.9 collective-permute-start.5
  18.7 2.6 collective-permute-start.15
  21.3 32.9 %collective-permute-done.5 = bf16[2,64,512]{2,1,0:T(8,128)(2,1)S(1)} collective-permute-done((bf16[2,64,512]{2,1,0:T(8,128)(2,1)S(1)}, bf16[2,64,512]{2,1,0:T(8,128)(2,1)S(1)}, u32[]{:S(2)}, u32[]{:S(2)}) %collective-permute-start.5) | collective-permute-done | bytes 131104 | tf_op jit(solution)/shard_map/ppermute | solution.py:22
  55.1 7.6 %collective-permute-done.20 = bf16[2,96,512]{2,1,0:T(8,128)(2,1)S(1)} collective-permute-done((bf16[2,96,512]{2,1,0:T(8,128)(2,1)S(1)}, bf16[2,96,512]{2,1,0:T(8,128)(2,1)S(1)}, u32[]{:S(2)}, u32[]{:S(2)}) %collective-permute-start.20) | collective-permute-done | bytes 196640 | tf_op jit(solution)/shard_map/ppermute | solution.py:22
  64.2 2.7 collective-permute-done.15
  66.9 3.1 collective-permute-done.10
  74.8 4.8 %collective-permute-done.3.refs_2_ = bf16[2,32,2048]{2,1,0:T(8,128)(2,1)S(1)} collective-permute-done((bf16[2,32,2048]{2,1,0:T(8,128)(2,1)S(1)}, bf16[2,32,2048]{2,1,0:T(8,128)(2,1)S(1)}, u32[]{:S(2)}, u32[]{:S(2)}) %collective-permute-start.3) | collective-permute-done | bytes 262176 | tf_op jit(solution)/shard_map/ppermute | solution.py:22
  81.8 13.9 %collective-permute-done.37 = bf16[2,512,256]{2,1,0:T(8,128)(2,1)S(1)} collective-permute-done((bf16[2,512,256]{2,1,0:T(8,128)(2,1)S(1)}, bf16[2,512,256]{2,1,0:T(8,128)(2,1)S(1)}, u32[]{:S(2)}, u32[]{:S(2)}) %collective-permute-start.37) | collective-permute-done | bytes 524320 | tf_op jit(solution)/shard_map/ppermute | solution.py:22
  97.0 9.2 %collective-permute-start.16 = (bf16[2,96,1024]{2,1,0:T(8,128)(2,1)S(1)}, bf16[2,96,1024]{2,1,0:T(8,128)(2,1)S(1)}, u32[]{:S(2)}, u32[]{:S(2)}) collective-permute-start(bf16[2,96,1024]{2,1,0:T(8,128)(2,1)S(1)} %pad_maximum_fusion.7), channel_id=1, source_target_pairs={{0,1},{1,0},{2,3},{3,2},{4,5},{5,4},{6,7},{7,6},{8,9},{9,8},{10,11... | collective-permute-start | bytes 1179656 | tf_op jit(solution)/shard_map/ppermute | solution.py:22
  106.3 10.7 %collective-permute-done.25 = bf16[2,512,256]{2,1,0:T(8,128)(2,1)S(1)} collective-permute-done((bf16[2,512,256]{2,1,0:T(8,128)(2,1)S(1)}, bf16[2,512,256]{2,1,0:T(8,128)(2,1)S(1)}, u32[]{:S(2)}, u32[]{:S(2)}) %collective-permute-start.25) | collective-permute-done | bytes 524320 | tf_op jit(solution)/shard_map/ppermute | solution.py:22
  118.5 19.3 %collective-permute-done.26 = bf16[2,512,256]{2,1,0:T(8,128)(2,1)S(1)} collective-permute-done((bf16[2,512,256]{2,1,0:T(8,128)(2,1)S(1)}, bf16[2,512,256]{2,1,0:T(8,128)(2,1)S(1)}, u32[]{:S(2)}, u32[]{:S(2)}) %collective-permute-start.26) | collective-permute-done | bytes 524320 | tf_op jit(solution)/shard_map/ppermute | solution.py:22
  139.3 6.9 %collective-permute-done.16 = bf16[2,96,1024]{2,1,0:T(8,128)(2,1)S(1)} collective-permute-done((bf16[2,96,1024]{2,1,0:T(8,128)(2,1)S(1)}, bf16[2,96,1024]{2,1,0:T(8,128)(2,1)S(1)}, u32[]{:S(2)}, u32[]{:S(2)}) %collective-permute-start.16) | collective-permute-done | bytes 393248 | tf_op jit(solution)/shard_map/ppermute | solution.py:22
  149.4 3.7 %collective-permute-done.11 = bf16[2,96,1024]{2,1,0:T(8,128)(2,1)S(1)} collective-permute-done((bf16[2,96,1024]{2,1,0:T(8,128)(2,1)S(1)}, bf16[2,96,1024]{2,1,0:T(8,128)(2,1)S(1)}, u32[]{:S(2)}, u32[]{:S(2)}) %collective-permute-start.11) | collective-permute-done | bytes 393248 | tf_op jit(solution)/shard_map/ppermute | solution.py:22
  159.8 8.7 %collective-permute-done.22.refs_17_ = bf16[2,96,2048]{2,1,0:T(8,128)(2,1)} collective-permute-done((bf16[2,96,2048]{2,1,0:T(8,128)(2,1)S(1)}, bf16[2,96,2048]{2,1,0:T(8,128)(2,1)}, u32[]{:S(2)}, u32[]{:S(2)}) %collective-permute-start.22) | collective-permute-done | bytes 786464 | tf_op jit(solution)/shard_map/ppermute | solution.py:22
  169.9 3.7 %collective-permute-done.18.refs_14_ = bf16[2,96,2048]{2,1,0:T(8,128)(2,1)} collective-permute-done((bf16[2,96,2048]{2,1,0:T(8,128)(2,1)S(1)}, bf16[2,96,2048]{2,1,0:T(8,128)(2,1)}, u32[]{:S(2)}, u32[]{:S(2)}) %collective-permute-start.18) | collective-permute-done | bytes 786464 | tf_op jit(solution)/shard_map/ppermute | solution.py:22
  175.3 10.0 %collective-permute-done.12.refs_9_ = bf16[2,96,2048]{2,1,0:T(8,128)(2,1)} collective-permute-done((bf16[2,96,2048]{2,1,0:T(8,128)(2,1)S(1)}, bf16[2,96,2048]{2,1,0:T(8,128)(2,1)}, u32[]{:S(2)}, u32[]{:S(2)}) %collective-permute-start.12) | collective-permute-done | bytes 786464 | tf_op jit(solution)/shard_map/ppermute | solution.py:22
  185.3 5.0 %collective-permute-done.23.refs_18_ = bf16[2,96,2048]{2,1,0:T(8,128)(2,1)S(1)} collective-permute-done((bf16[2,96,2048]{2,1,0:T(8,128)(2,1)S(1)}, bf16[2,96,2048]{2,1,0:T(8,128)(2,1)S(1)}, u32[]{:S(2)}, u32[]{:S(2)}) %collective-permute-start.23) | collective-permute-done | bytes 786464 | tf_op jit(solution)/shard_map/ppermute | solution.py:22
  192.8 9.2 %collective-permute-done.17.refs_13_ = bf16[2,96,2048]{2,1,0:T(8,128)(2,1)S(1)} collective-permute-done((bf16[2,96,2048]{2,1,0:T(8,128)(2,1)S(1)}, bf16[2,96,2048]{2,1,0:T(8,128)(2,1)S(1)}, u32[]{:S(2)}, u32[]{:S(2)}) %collective-permute-start.17) | collective-permute-done | bytes 786464 | tf_op jit(solution)/shard_map/ppermute | solution.py:22
  204.0 3.2 collective-permute-done.13.refs_10_
  209.6 3.7 %collective-permute-done.9.refs_7_ = bf16[2,64,2048]{2,1,0:T(8,128)(2,1)S(1)} collective-permute-done((bf16[2,64,2048]{2,1,0:T(8,128)(2,1)S(1)}, bf16[2,64,2048]{2,1,0:T(8,128)(2,1)S(1)}, u32[]{:S(2)}, u32[]{:S(2)}) %collective-permute-start.9) | collective-permute-done | bytes 524320 | tf_op jit(solution)/shard_map/ppermute | solution.py:22
  215.8 4.2 %all-to-all-start = ((f32[4,27,384]{2,1,0:T(8,128)}), f32[4,27,384]{2,1,0:T(8,128)}, u32[]{:S(2)}, u32[]{:S(2)}) async-start(f32[4,27,384]{2,1,0:T(8,128)} %broadcast_in_dim.27), calls=%async_computation | async-start | bytes 393216 | tf_op jit(solution)/shard_map/all_to_all | solution.py:28
  222.6 18.0 %all-to-all-done = f32[4,27,384]{2,1,0:T(8,128)} async-done(((f32[4,27,384]{2,1,0:T(8,128)}), f32[4,27,384]{2,1,0:T(8,128)}, u32[]{:S(2)}, u32[]{:S(2)}) %all-to-all-start) | async-done | bytes 165920 | tf_op jit(solution)/shard_map/all_to_all | solution.py:28
  257.4 10.2 %shard_map.113 = (bf16[4,384,256]{2,1,0:T(8,128)(2,1)S(1)}, bf16[4,384,256]{2,1,0:T(8,128)(2,1)S(1)}, f32[4,8,384]{2,1,0:T(8,128)S(1)}, f32[4,24,384]{2,1,0:T(8,128)S(1)}) custom-call(s32[1]{0:T(128)} %bitcast.1.row_ref, bf16[2,32,2048]{2,1,0:T(8,128)(2,1)S(1)} %pad_maximum_fusion.9.refs_0_, bf16[2,32,2048]{2,1,0:T(8,128)(2,1)S(1)} %copy-done.42, ...), custom_call_target="tpu_custom_call" | custom-call | flops 6442450944 | bytes 12582912 | tf_op jit(solution)/shard_map/pallas_call | solution.py:95
  273.7 4.6 %all-to-all-start.1 = ((f32[16,25,96]{2,1,0:T(8,128)}), f32[16,25,96]{2,1,0:T(8,128)}, u32[]{:S(2)}, u32[]{:S(2)}) async-start(f32[16,25,96]{2,1,0:T(8,128)} %copy.38), calls=%async_computation.1 | async-start | bytes 524288 | tf_op jit(solution)/shard_map/all_to_all | solution.py:272
  293.4 10.3 %shard_map.112 = (bf16[4,384,256]{2,1,0:T(8,128)(2,1)S(1)}, bf16[4,384,256]{2,1,0:T(8,128)(2,1)S(1)}, f32[4,8,384]{2,1,0:T(8,128)S(1)}, f32[4,8,384]{2,1,0:T(8,128)S(1)}) custom-call(s32[1]{0:T(128)} %bitcast.1.row_ref, bf16[2,32,2048]{2,1,0:T(8,128)(2,1)S(1)} %pad_maximum_fusion.9.refs_0_, bf16[2,32,2048]{2,1,0:T(8,128)(2,1)S(1)} %copy-done.43, ...), custom_call_target="tpu_custom_call" | custom-call | flops 6442450944 | bytes 12582912 | tf_op jit(solution)/shard_map/pallas_call | solution.py:95
  312.1 3.3 collective-permute-done.31
  319.6 3.7 %all-to-all-start.2 = ((f32[16,26,96]{2,1,0:T(8,128)}), f32[16,26,96]{2,1,0:T(8,128)S(1)}, u32[]{:S(2)}, u32[]{:S(2)}) async-start(f32[16,26,96]{2,1,0:T(8,128)} %broadcast_in_dim.28), calls=%async_computation.2 | async-start | bytes 524288 | tf_op jit(solution)/shard_map/all_to_all | solution.py:28
  324.8 7.8 %all-to-all-done.2 = f32[16,26,96]{2,1,0:T(8,128)S(1)} async-done(((f32[16,26,96]{2,1,0:T(8,128)}), f32[16,26,96]{2,1,0:T(8,128)S(1)}, u32[]{:S(2)}, u32[]{:S(2)}) %all-to-all-start.2) | async-done | bytes 159776 | tf_op jit(solution)/shard_map/all_to_all | solution.py:28
  336.5 2.6 all-to-all-start.3
  339.8 15.7 %all-to-all-done.3 = bf16[32,29,256]{2,1,0:T(8,128)(2,1)S(1)} async-done(((bf16[32,29,256]{2,1,0:T(8,128)(2,1)}), bf16[32,29,256]{2,1,0:T(8,128)(2,1)S(1)}, u32[]{:S(2)}, u32[]{:S(2)}) %all-to-all-start.3) | async-done | bytes 475168 | tf_op jit(solution)/shard_map/all_to_all | solution.py:300
  (237 shorter events, 101.1 us)
Async XLA Ops:
  13.5 66.2 %collective-permute-start.36 = (bf16[2,512,256]{2,1,0:T(8,128)(2,1)S(1)}, bf16[2,512,256]{2,1,0:T(8,128)(2,1)S(1)}, u32[]{:S(2)}, u32[]{:S(2)}) collective-permute-start(bf16[2,512,256]{2,1,0:T(8,128)(2,1)S(1)} %get-tuple-element.24), channel_id=1, source_target_pairs={{0,2},{1,3},{2,0},{3,1},{4,6},{5,7},{6,4},{7,5},{8,10},{9,11},{10,... | collective-permute-start | bytes 1572872 | tf_op jit(solution)/shard_map/ppermute | solution.py:22
  13.6 40.6 %collective-permute-start.5 = (bf16[2,64,512]{2,1,0:T(8,128)(2,1)S(1)}, bf16[2,64,512]{2,1,0:T(8,128)(2,1)S(1)}, u32[]{:S(2)}, u32[]{:S(2)}) collective-permute-start(bf16[2,64,512]{2,1,0:T(8,128)(2,1)S(1)} %slice.71), channel_id=1, source_target_pairs={{0,2},{1,3},{2,0},{3,1},{4,6},{5,7},{6,4},{7,5},{8,10},{9,11},{10,... | collective-permute-start | bytes 393224 | tf_op jit(solution)/shard_map/ppermute | solution.py:22
  16.6 37.7 %collective-permute-start.1 = (bf16[2,32,1024]{2,1,0:T(8,128)(2,1)S(1)}, bf16[2,32,1024]{2,1,0:T(8,128)(2,1)S(1)}, u32[]{:S(2)}, u32[]{:S(2)}) collective-permute-start(bf16[2,32,1024]{2,1,0:T(8,128)(2,1)S(1)} %pad_maximum_fusion.11), channel_id=1, source_target_pairs={{0,1},{1,0},{2,3},{3,2},{4,5},{5,4},{6,7},{7,6},{8,9},{9,8},{10,11... | collective-permute-start | bytes 393224 | tf_op jit(solution)/shard_map/ppermute | solution.py:22
  18.3 44.4 %collective-permute-start.20 = (bf16[2,96,512]{2,1,0:T(8,128)(2,1)S(1)}, bf16[2,96,512]{2,1,0:T(8,128)(2,1)S(1)}, u32[]{:S(2)}, u32[]{:S(2)}) collective-permute-start(bf16[2,96,512]{2,1,0:T(8,128)(2,1)S(1)} %get-tuple-element.31), channel_id=1, source_target_pairs={{0,2},{1,3},{2,0},{3,1},{4,6},{5,7},{6,4},{7,5},{8,10},{9,11},{10,... | collective-permute-start | bytes 589832 | tf_op jit(solution)/shard_map/ppermute | solution.py:22
  18.7 48.3 %collective-permute-start.15 = (bf16[2,96,512]{2,1,0:T(8,128)(2,1)S(1)}, bf16[2,96,512]{2,1,0:T(8,128)(2,1)S(1)}, u32[]{:S(2)}, u32[]{:S(2)}) collective-permute-start(bf16[2,96,512]{2,1,0:T(8,128)(2,1)S(1)} %get-tuple-element.32), channel_id=1, source_target_pairs={{0,2},{1,3},{2,0},{3,1},{4,6},{5,7},{6,4},{7,5},{8,10},{9,11},{10,... | collective-permute-start | bytes 589832 | tf_op jit(solution)/shard_map/ppermute | solution.py:22
  54.2 15.8 %collective-permute-start.10 = (bf16[2,96,512]{2,1,0:T(8,128)(2,1)S(1)}, bf16[2,96,512]{2,1,0:T(8,128)(2,1)S(1)}, u32[]{:S(2)}, u32[]{:S(2)}) collective-permute-start(bf16[2,96,512]{2,1,0:T(8,128)(2,1)S(1)} %get-tuple-element.33), channel_id=1, source_target_pairs={{0,2},{1,3},{2,0},{3,1},{4,6},{5,7},{6,4},{7,5},{8,10},{9,11},{10,... | collective-permute-start | bytes 589832 | tf_op jit(solution)/shard_map/ppermute | solution.py:22
  54.2 19.0 %collective-permute-start.6 = (bf16[2,64,1024]{2,1,0:T(8,128)(2,1)S(1)}, bf16[2,64,1024]{2,1,0:T(8,128)(2,1)S(1)}, u32[]{:S(2)}, u32[]{:S(2)}) collective-permute-start(bf16[2,64,1024]{2,1,0:T(8,128)(2,1)S(1)} %pad_maximum_fusion.10), channel_id=1, source_target_pairs={{0,1},{1,0},{2,3},{3,2},{4,5},{5,4},{6,7},{7,6},{8,9},{9,8},{10,11... | collective-permute-start | bytes 786440 | tf_op jit(solution)/shard_map/ppermute | solution.py:22
  66.9 28.8 %collective-permute-start.37 = (bf16[2,512,256]{2,1,0:T(8,128)(2,1)S(1)}, bf16[2,512,256]{2,1,0:T(8,128)(2,1)S(1)}, u32[]{:S(2)}, u32[]{:S(2)}) collective-permute-start(bf16[2,512,256]{2,1,0:T(8,128)(2,1)S(1)} %get-tuple-element.30), channel_id=1, source_target_pairs={{0,1},{1,0},{2,3},{3,2},{4,5},{5,4},{6,7},{7,6},{8,9},{9,8},{10,11... | collective-permute-start | bytes 1572872 | tf_op jit(solution)/shard_map/ppermute | solution.py:22
  70.0 27.0 %collective-permute-start.38 = (bf16[2,512,256]{2,1,0:T(8,128)(2,1)S(1)}, bf16[2,512,256]{2,1,0:T(8,128)(2,1)S(1)}, u32[]{:S(2)}, u32[]{:S(2)}) collective-permute-start(bf16[2,512,256]{2,1,0:T(8,128)(2,1)S(1)} %get-tuple-element.29), channel_id=1, source_target_pairs={{0,3},{1,2},{2,1},{3,0},{4,7},{5,6},{6,5},{7,4},{8,11},{9,10},{10,... | collective-permute-start | bytes 1572872 | tf_op jit(solution)/shard_map/ppermute | solution.py:22
  74.7 42.2 %collective-permute-start.25 = (bf16[2,512,256]{2,1,0:T(8,128)(2,1)S(1)}, bf16[2,512,256]{2,1,0:T(8,128)(2,1)S(1)}, u32[]{:S(2)}, u32[]{:S(2)}) collective-permute-start(bf16[2,512,256]{2,1,0:T(8,128)(2,1)S(1)} %get-tuple-element.27), channel_id=1, source_target_pairs={{0,2},{1,3},{2,0},{3,1},{4,6},{5,7},{6,4},{7,5},{8,10},{9,11},{10,... | collective-permute-start | bytes 1572872 | tf_op jit(solution)/shard_map/ppermute | solution.py:22
  79.6 37.4 %collective-permute-start.21 = (bf16[2,96,1024]{2,1,0:T(8,128)(2,1)S(1)}, bf16[2,96,1024]{2,1,0:T(8,128)(2,1)S(1)}, u32[]{:S(2)}, u32[]{:S(2)}) collective-permute-start(bf16[2,96,1024]{2,1,0:T(8,128)(2,1)S(1)} %pad_maximum_fusion.8), channel_id=1, source_target_pairs={{0,1},{1,0},{2,3},{3,2},{4,5},{5,4},{6,7},{7,6},{8,9},{9,8},{10,11... | collective-permute-start | bytes 1179656 | tf_op jit(solution)/shard_map/ppermute | solution.py:22
  79.6 58.2 %collective-permute-start.26 = (bf16[2,512,256]{2,1,0:T(8,128)(2,1)S(1)}, bf16[2,512,256]{2,1,0:T(8,128)(2,1)S(1)}, u32[]{:S(2)}, u32[]{:S(2)}) collective-permute-start(bf16[2,512,256]{2,1,0:T(8,128)(2,1)S(1)} %get-tuple-element.26), channel_id=1, source_target_pairs={{0,1},{1,0},{2,3},{3,2},{4,5},{5,4},{6,7},{7,6},{8,9},{9,8},{10,11... | collective-permute-start | bytes 1572872 | tf_op jit(solution)/shard_map/ppermute | solution.py:22
  95.7 52.2 %collective-permute-start.27 = (bf16[2,512,256]{2,1,0:T(8,128)(2,1)S(1)}, bf16[2,512,256]{2,1,0:T(8,128)(2,1)S(1)}, u32[]{:S(2)}, u32[]{:S(2)}) collective-permute-start(bf16[2,512,256]{2,1,0:T(8,128)(2,1)S(1)} %get-tuple-element.25), channel_id=1, source_target_pairs={{0,3},{1,2},{2,1},{3,0},{4,7},{5,6},{6,5},{7,4},{8,11},{9,10},{10,... | collective-permute-start | bytes 1572872 | tf_op jit(solution)/shard_map/ppermute | solution.py:22
  97.0 49.2 %collective-permute-start.16 = (bf16[2,96,1024]{2,1,0:T(8,128)(2,1)S(1)}, bf16[2,96,1024]{2,1,0:T(8,128)(2,1)S(1)}, u32[]{:S(2)}, u32[]{:S(2)}) collective-permute-start(bf16[2,96,1024]{2,1,0:T(8,128)(2,1)S(1)} %pad_maximum_fusion.7), channel_id=1, source_target_pairs={{0,1},{1,0},{2,3},{3,2},{4,5},{5,4},{6,7},{7,6},{8,9},{9,8},{10,11... | collective-permute-start | bytes 1179656 | tf_op jit(solution)/shard_map/ppermute | solution.py:22
  116.9 36.1 %collective-permute-start.11 = (bf16[2,96,1024]{2,1,0:T(8,128)(2,1)S(1)}, bf16[2,96,1024]{2,1,0:T(8,128)(2,1)S(1)}, u32[]{:S(2)}, u32[]{:S(2)}) collective-permute-start(bf16[2,96,1024]{2,1,0:T(8,128)(2,1)S(1)} %pad_maximum_fusion.6), channel_id=1, source_target_pairs={{0,1},{1,0},{2,3},{3,2},{4,5},{5,4},{6,7},{7,6},{8,9},{9,8},{10,11... | collective-permute-start | bytes 1179656 | tf_op jit(solution)/shard_map/ppermute | solution.py:22
  116.9 39.0 %collective-permute-start.8 = (bf16[2,64,2048]{2,1,0:T(8,128)(2,1)S(1)}, bf16[2,64,2048]{2,1,0:T(8,128)(2,1)S(1)}, u32[]{:S(2)}, u32[]{:S(2)}) collective-permute-start(bf16[2,64,2048]{2,1,0:T(8,128)(2,1)S(1)} %pad_maximum_fusion.5.refs_4_), channel_id=1, source_target_pairs={{0,8},{4,12},{8,0},{12,4},{1,9},{5,13},{9,1},{13,5},{2,10},{6,14},... | collective-permute-start | bytes 1572872 | tf_op jit(solution)/shard_map/ppermute | solution.py:22
  137.8 21.1 %collective-permute-start.7 = (bf16[2,64,2048]{2,1,0:T(8,128)(2,1)S(1)}, bf16[2,64,2048]{2,1,0:T(8,128)(2,1)S(1)}, u32[]{:S(2)}, u32[]{:S(2)}) collective-permute-start(bf16[2,64,2048]{2,1,0:T(8,128)(2,1)S(1)} %pad_maximum_fusion.5.refs_4_), channel_id=1, source_target_pairs={{0,4},{4,0},{8,12},{12,8},{1,5},{5,1},{9,13},{13,9},{2,6},{6,2},{1... | collective-permute-start | bytes 1572872 | tf_op jit(solution)/shard_map/ppermute | solution.py:22
  147.9 20.6 %collective-permute-start.22 = (bf16[2,96,2048]{2,1,0:T(8,128)(2,1)S(1)}, bf16[2,96,2048]{2,1,0:T(8,128)(2,1)}, u32[]{:S(2)}, u32[]{:S(2)}) collective-permute-start(bf16[2,96,2048]{2,1,0:T(8,128)(2,1)S(1)} %pad_maximum_fusion.4.refs_16_), channel_id=1, source_target_pairs={{0,4},{4,0},{8,12},{12,8},{1,5},{5,1},{9,13},{13,9},{2,6},{6,2},{1... | collective-permute-start | bytes 2359304 | tf_op jit(solution)/shard_map/ppermute | solution.py:22
  153.1 20.5 %collective-permute-start.18 = (bf16[2,96,2048]{2,1,0:T(8,128)(2,1)S(1)}, bf16[2,96,2048]{2,1,0:T(8,128)(2,1)}, u32[]{:S(2)}, u32[]{:S(2)}) collective-permute-start(bf16[2,96,2048]{2,1,0:T(8,128)(2,1)S(1)} %pad_maximum_fusion.3.refs_12_), channel_id=1, source_target_pairs={{0,8},{4,12},{8,0},{12,4},{1,9},{5,13},{9,1},{13,5},{2,10},{6,14},... | collective-permute-start | bytes 2359304 | tf_op jit(solution)/shard_map/ppermute | solution.py:22
  155.5 34.9 %collective-permute-start.23 = (bf16[2,96,2048]{2,1,0:T(8,128)(2,1)S(1)}, bf16[2,96,2048]{2,1,0:T(8,128)(2,1)S(1)}, u32[]{:S(2)}, u32[]{:S(2)}) collective-permute-start(bf16[2,96,2048]{2,1,0:T(8,128)(2,1)S(1)} %pad_maximum_fusion.4.refs_16_), channel_id=1, source_target_pairs={{0,8},{4,12},{8,0},{12,4},{1,9},{5,13},{9,1},{13,5},{2,10},{6,14},... | collective-permute-start | bytes 2359304 | tf_op jit(solution)/shard_map/ppermute | solution.py:22
  156.0 29.3 %collective-permute-start.12 = (bf16[2,96,2048]{2,1,0:T(8,128)(2,1)S(1)}, bf16[2,96,2048]{2,1,0:T(8,128)(2,1)}, u32[]{:S(2)}, u32[]{:S(2)}) collective-permute-start(bf16[2,96,2048]{2,1,0:T(8,128)(2,1)S(1)} %pad_maximum_fusion.2.refs_8_), channel_id=1, source_target_pairs={{0,4},{4,0},{8,12},{12,8},{1,5},{5,1},{9,13},{13,9},{2,6},{6,2},{1... | collective-permute-start | bytes 2359304 | tf_op jit(solution)/shard_map/ppermute | solution.py:22
  159.7 84.3 %collective-permute-start.39 = (bf16[2,2048,256]{2,1,0:T(8,128)(2,1)}, bf16[2,2048,256]{2,1,0:T(8,128)(2,1)}, u32[]{:S(2)}, u32[]{:S(2)}) collective-permute-start(bf16[2,2048,256]{2,1,0:T(8,128)(2,1)} %pad_maximum_fusion.1.refs_20_), channel_id=1, source_target_pairs={{0,16},{16,0},{1,17},{17,1},{2,18},{18,2},{3,19},{19,3},{4,20},{20... | collective-permute-start | bytes 6291464 | tf_op jit(solution)/shard_map/ppermute | solution.py:22
  168.5 33.6 %collective-permute-start.17 = (bf16[2,96,2048]{2,1,0:T(8,128)(2,1)S(1)}, bf16[2,96,2048]{2,1,0:T(8,128)(2,1)S(1)}, u32[]{:S(2)}, u32[]{:S(2)}) collective-permute-start(bf16[2,96,2048]{2,1,0:T(8,128)(2,1)S(1)} %pad_maximum_fusion.3.refs_12_), channel_id=1, source_target_pairs={{0,4},{4,0},{8,12},{12,8},{1,5},{5,1},{9,13},{13,9},{2,6},{6,2},{1... | collective-permute-start | bytes 2359304 | tf_op jit(solution)/shard_map/ppermute | solution.py:22
  173.6 33.6 %collective-permute-start.13 = (bf16[2,96,2048]{2,1,0:T(8,128)(2,1)S(1)}, bf16[2,96,2048]{2,1,0:T(8,128)(2,1)S(1)}, u32[]{:S(2)}, u32[]{:S(2)}) collective-permute-start(bf16[2,96,2048]{2,1,0:T(8,128)(2,1)S(1)} %pad_maximum_fusion.2.refs_8_), channel_id=1, source_target_pairs={{0,8},{4,12},{8,0},{12,4},{1,9},{5,13},{9,1},{13,5},{2,10},{6,14},... | collective-permute-start | bytes 2359304 | tf_op jit(solution)/shard_map/ppermute | solution.py:22
  185.3 93.0 %collective-permute-start.28 = (bf16[2,2048,256]{2,1,0:T(8,128)(2,1)S(1)}, bf16[2,2048,256]{2,1,0:T(8,128)(2,1)}, u32[]{:S(2)}, u32[]{:S(2)}) collective-permute-start(bf16[2,2048,256]{2,1,0:T(8,128)(2,1)S(1)} %pad_maximum_fusion.refs_20_), channel_id=1, source_target_pairs={{0,16},{16,0},{1,17},{17,1},{2,18},{18,2},{3,19},{19,3},{4,20},{20... | collective-permute-start | bytes 6291464 | tf_op jit(solution)/shard_map/ppermute | solution.py:22
  191.3 22.0 %collective-permute-start.9 = (bf16[2,64,2048]{2,1,0:T(8,128)(2,1)S(1)}, bf16[2,64,2048]{2,1,0:T(8,128)(2,1)S(1)}, u32[]{:S(2)}, u32[]{:S(2)}) collective-permute-start(bf16[2,64,2048]{2,1,0:T(8,128)(2,1)S(1)} %collective-permute-done.8.refs_6_), channel_id=1, source_target_pairs={{0,4},{4,0},{8,12},{12,8},{1,5},{5,1},{9,13},{13,9},{2,6},{6,2},{1... | collective-permute-start | bytes 1572872 | tf_op jit(solution)/shard_map/ppermute | solution.py:22
  203.0 41.1 %collective-permute-start.24 = (bf16[2,96,2048]{2,1,0:T(8,128)(2,1)}, bf16[2,96,2048]{2,1,0:T(8,128)(2,1)}, u32[]{:S(2)}, u32[]{:S(2)}) collective-permute-start(bf16[2,96,2048]{2,1,0:T(8,128)(2,1)} %collective-permute-done.22.refs_17_), channel_id=1, source_target_pairs={{0,8},{4,12},{8,0},{12,4},{1,9},{5,13},{9,1},{13,5},{2,10},{6,14},... | collective-permute-start | bytes 2359304 | tf_op jit(solution)/shard_map/ppermute | solution.py:22
  208.1 36.0 %collective-permute-start.19 = (bf16[2,96,2048]{2,1,0:T(8,128)(2,1)}, bf16[2,96,2048]{2,1,0:T(8,128)(2,1)}, u32[]{:S(2)}, u32[]{:S(2)}) collective-permute-start(bf16[2,96,2048]{2,1,0:T(8,128)(2,1)} %collective-permute-done.18.refs_14_), channel_id=1, source_target_pairs={{0,4},{4,0},{8,12},{12,8},{1,5},{5,1},{9,13},{13,9},{2,6},{6,2},{1... | collective-permute-start | bytes 2359304 | tf_op jit(solution)/shard_map/ppermute | solution.py:22
  214.1 30.0 %collective-permute-start.14 = (bf16[2,96,2048]{2,1,0:T(8,128)(2,1)}, bf16[2,96,2048]{2,1,0:T(8,128)(2,1)}, u32[]{:S(2)}, u32[]{:S(2)}) collective-permute-start(bf16[2,96,2048]{2,1,0:T(8,128)(2,1)} %collective-permute-done.12.refs_9_), channel_id=1, source_target_pairs={{0,8},{4,12},{8,0},{12,4},{1,9},{5,13},{9,1},{13,5},{2,10},{6,14},... | collective-permute-start | bytes 2359304 | tf_op jit(solution)/shard_map/ppermute | solution.py:22
  215.8 24.9 %all-to-all-start = ((f32[4,27,384]{2,1,0:T(8,128)}), f32[4,27,384]{2,1,0:T(8,128)}, u32[]{:S(2)}, u32[]{:S(2)}) async-start(f32[4,27,384]{2,1,0:T(8,128)} %broadcast_in_dim.27), calls=%async_computation | async-start | bytes 393216 | tf_op jit(solution)/shard_map/all_to_all | solution.py:28
  273.7 36.3 %all-to-all-start.1 = ((f32[16,25,96]{2,1,0:T(8,128)}), f32[16,25,96]{2,1,0:T(8,128)}, u32[]{:S(2)}, u32[]{:S(2)}) async-start(f32[16,25,96]{2,1,0:T(8,128)} %copy.38), calls=%async_computation.1 | async-start | bytes 524288 | tf_op jit(solution)/shard_map/all_to_all | solution.py:272
  336.5 18.9 %all-to-all-start.3 = ((bf16[32,29,256]{2,1,0:T(8,128)(2,1)}), bf16[32,29,256]{2,1,0:T(8,128)(2,1)S(1)}, u32[]{:S(2)}, u32[]{:S(2)}) async-start(bf16[32,29,256]{2,1,0:T(8,128)(2,1)} %copy-done.18), calls=%async_computation.3 | async-start | bytes 1048576 | tf_op jit(solution)/shard_map/all_to_all | solution.py:300
  (69 other events, 798.3 us)

commit v2 on v1

--- a/solution.py
+++ b/solution.py
@@ -12,7 +12,6 @@
 GAMMA = 0.99
 TAU = 0.7
 FLOOR = 0.01
-ORDER = (3, 2, 0, 1)
 F32 = jnp.float32
 BF16 = jnp.bfloat16
 
@@ -32,7 +31,8 @@
     return [1 << b for b in range(size.bit_length() - 1)]
 
 
-def net_kernel(row_ref, *refs, places, row_count, nets, with_actions):
+def net_kernel(row_ref, *refs, places, row_count, picks, with_actions):
+    nets = len(picks)
     count = len(places)
     pieces = refs[:count]
     own_ref, other_ref = refs[count : count + 2]
@@ -43,8 +43,8 @@
         act_ref, act_w_ref = refs[at : at + 2]
         at += 2
     hidden_refs = refs[at : at + nets]
-    part_refs = refs[at + nets : at + 2 * nets]
-    buf, w_buf, sems, w_sems = refs[at + 2 * nets :]
+    part_ref, buf, w_buf, sems, w_sems = refs[at + nets :]
+    rows = buf.shape[2]
     w_copies = [
         pltpu.make_async_copy(ref, w_buf.at[i], w_sems.at[i])
         for i, ref in enumerate((own_ref, other_ref))
@@ -69,21 +69,27 @@
                 copies[i].wait()
         where = jnp.bitwise_xor(row, j)
         for n in range(nets):
-            acc = jnp.dot(buf[j, 0], w_buf[0, n], preferred_element_type=F32)
-            acc = acc + jnp.dot(buf[j, 1], w_buf[1, n], preferred_element_type=F32)
+            acc = jnp.dot(buf[j, 0], w_buf[0, picks[n]], preferred_element_type=F32)
+            acc = acc + jnp.dot(buf[j, 1], w_buf[1, picks[n]], preferred_element_type=F32)
             if with_actions:
                 acc = acc + jnp.dot(act_ref[where], act_w_ref[n], preferred_element_type=F32)
             hidden = jnp.maximum(acc, 0.0).astype(BF16)
             hidden_refs[n][where] = hidden
-    for n in range(nets):
-        for j in range(row_count):
-            part_refs[n][j] = lax.dot_general(
+    for j in range(row_count):
+        at = 0
+        for n in range(nets):
+            part = lax.dot_general(
                 head_refs[n][...], hidden_refs[n][j], (((1,), (1,)), ((), ())),
                 preferred_element_type=F32,
             )
-
-
-def run_nets(row_at, pieces, places, w_own, w_other, heads, rows, row_count, extra):
+            if with_actions:
+                part_ref[n : n + 1, j * rows : (j + 1) * rows] = part[0:1]
+            else:
+                part_ref[j, at : at + part.shape[0], :] = part
+            at += part.shape[0]
+
+
+def run_nets(row_at, pieces, places, w_own, w_other, heads, rows, row_count, extra, picks):
     nets, depth, units = w_own.shape
     any_spec = pl.BlockSpec(memory_space=pl.ANY)
     vmem = pl.BlockSpec(memory_space=pltpu.VMEM)
@@ -91,18 +97,18 @@
     late = [w_own, w_other, *heads, *extra]
     tokens = row_count * rows
     wide = max(units, 128)
-    held = 4 * tokens * depth + 8 * nets * depth * wide + 4 * nets * tokens * wide
+    held = 4 * tokens * depth + 4 * nets * depth * wide + 2 * nets * tokens * wide
     outs = pl.pallas_call(
         functools.partial(
-            net_kernel, places=places, row_count=row_count, nets=nets,
+            net_kernel, places=places, row_count=row_count, picks=picks,
             with_actions=bool(extra),
         ),
         out_shape=tuple(
             [jax.ShapeDtypeStruct((row_count, rows, units), BF16)] * nets
-            + [jax.ShapeDtypeStruct((row_count, h.shape[0], rows), F32) for h in heads]
+            + [jax.ShapeDtypeStruct((nets, tokens) if extra else (row_count, 32, rows), F32)]
         ),
         in_specs=[smem] + [any_spec] * (len(pieces) + 2) + [vmem] * (len(late) - 2),
-        out_specs=tuple([vmem] * (2 * nets)),
+        out_specs=tuple([vmem] * (nets + 1)),
         scratch_shapes=[
             pltpu.VMEM((row_count, 2, rows, depth), BF16),
             pltpu.VMEM((2, nets, depth, units), BF16),
@@ -116,7 +122,7 @@
             transcendentals=0,
         ),
     )(row_at.reshape(1), *pieces, *late)
-    return outs[:nets], outs[nets:]
+    return outs[:nets], outs[nets]
 
 
 def split_dot(coeff, hidden):
@@ -126,10 +132,29 @@
     return out + jnp.dot(low, hidden, preferred_element_type=F32)
 
 
+def in_parts(coeff, first, last):
+    count, cut, _ = first.shape
+    size = cut + last.shape[1]
+    total = None
+    for j in range(count):
+        for ref, low, high in ((first, 0, cut), (last, cut, size)):
+            term = split_dot(coeff[:, j * size + low : j * size + high], ref[j])
+            total = term if total is None else total + term
+    return total
+
+
 def tail_kernel(
-    dp_ref, late_ref, pack_ref, known_ref, scale_ref, h0, h1, h2, h3,
-    adv_ref, out_ref, grad_ref, *, acts,
+    dp_ref, late_ref, pack_ref, known_ref, scale_ref, h0, h1, h2, h2_last, h3, h3_last,
+    adv_ref, out_ref, grad_ref, *rest, acts,
 ):
+    sources = (h0, h1, h2, h2_last, h3, h3_last)
+    copies = [
+        pltpu.make_async_copy(source, held, rest[-1].at[i])
+        for i, (source, held) in enumerate(zip(sources, rest[:-1]))
+    ]
+    for copy in copies:
+        copy.start()
+    h0, h1, h2, h2_last, h3, h3_last = rest[:-1]
     tokens = late_ref.shape[-1]
     dp = dp_ref[0]
     values = [known_ref[acts + d : acts + d + 1] for d in range(2)]
@@ -174,10 +199,12 @@
     high = loss.astype(BF16).astype(F32)
     grad_ref[acts + 3 : acts + 4] = high
     grad_ref[acts + 4 : acts + 5] = loss - high
+    for copy in copies:
+        copy.wait()
     grad_ref[0:1] = split_dot(2.0 * gap0, h0[...])
     grad_ref[1:2] = split_dot(2.0 * gap1, h1[...])
-    grad_ref[2:3] = split_dot(-2.0 * expectile * adv, h2[...])
-    grad_ref[3 : 3 + acts] = split_dot(-weight * scaled / scale, h3[...])
+    grad_ref[2:3] = in_parts(-2.0 * expectile * adv, h2, h2_last)
+    grad_ref[3 : 3 + acts] = in_parts(-weight * scaled / scale, h3, h3_last)
     out = grad_ref[...].astype(BF16)
     for i in range(out_ref.shape[0]):
         out_ref[i] = out
@@ -188,7 +215,7 @@
 ):
     rows, feats = states.shape
     acts = actions.shape[1]
-    nets, _, row_units = hidden_weights.shape
+    _, _, row_units = hidden_weights.shape
     row_count = lax.axis_size("row")
     col_count = lax.axis_size("col")
     dp_count = lax.axis_size("dp")
@@ -200,7 +227,7 @@
     half = feats // 2
     tokens = rows * row_count
     total = tokens * dp_count
-    shares = (1, 2, 3, 3, 3) if rows % 192 == 0 else (1,)
+    shares = (1, 3, 4, 3, 1) if rows % 192 == 0 else (1, 1)
     sizes = [rows * s // sum(shares) for s in shares]
     starts = [sum(sizes[:c]) for c in range(len(sizes))]
 
@@ -227,7 +254,8 @@
     for c, (start, size) in enumerate(zip(starts, sizes)):
         block = pair[:, start : start + size]
         for bit in col_bits:
-            block = jnp.concatenate([block, swap(block, "col", bit)], axis=2)
+            got = swap(block, "col", bit)
+            block = jnp.concatenate([block, got], axis=2)
         held = {0: block}
         order = bits_of(row_count)
         if c % 2:
@@ -239,62 +267,85 @@
             pieces.append(held[j])
             places.append((j, start, size))
 
-    hidden, parts = {}, {}
+    cut = rows * 2 // 3 if rows % 192 == 0 else starts[-1]
+    calls = [
+        [(p, (j, at, size)) for p, (j, at, size) in zip(pieces, places) if at < cut],
+        [(p, (j, at - cut, size)) for p, (j, at, size) in zip(pieces, places) if at >= cut],
+    ]
     unit_at = row_at * row_units + col_at * units
     heads_t = lax.dynamic_slice_in_dim(heads.T, unit_at, units, 1)
     act_w = lax.dynamic_slice_in_dim(action_weights, unit_at, units, 2)
-    for first in range(0, nets, 2):
-        group = ORDER[first : first + 2]
-        low = min(group)
-        mine = lax.dynamic_slice(
-            hidden_weights, (low, dp_at * half, 0), (len(group), half, row_units)
-        )
+    rest = jnp.zeros((7, units), heads.dtype)
+    head = [jnp.concatenate([heads_t[n : n + 1], rest], axis=0) for n in range(3)]
+    head.append(heads_t[3:])
+    exchanged = []
+    for first in (0, 2):
+        low = 2 - first
+        mine = lax.dynamic_slice(hidden_weights, (low, dp_at * half, 0), (2, half, row_units))
         got = []
         for k in cols:
             sent = lax.dynamic_slice_in_dim(mine, jnp.bitwise_xor(col_at, k) * units, units, 2)
-            got.append(swap(sent, "col", k) if k else sent)
+            if k == col_count - 1:
+                inner = {col_count // 2 - 1, col_count // 2}
+                near = [(i, i ^ k) for i in range(col_count) if i in inner]
+                far = [(i, i ^ k) for i in range(col_count) if i not in inner]
+                near = lax.ppermute(sent, "col", near)
+                far = lax.ppermute(sent, "col", far)
+                is_near = (col_at == col_count // 2 - 1) | (col_at == col_count // 2)
+                got.append(jnp.where(is_near, near, far))
+            else:
+                got.append(swap(sent, "col", k) if k else sent)
         w_own = jnp.concatenate(got, axis=1)
-        w_other = swap(w_own, "dp", 1)
-        group = range(low, low + len(group))
-        head = [
-            heads_t[3:] if n == 3 else jnp.pad(heads_t[n : n + 1], ((0, 7), (0, 0))) for n in group
-        ]
-        extra = (own_actions, act_w) if low == 0 else ()
-        got_hidden, got_parts = run_nets(
-            row_at, pieces, places, w_own, w_other, head, rows, row_count, extra
+        exchanged.append((w_own, swap(w_own, "dp", 1)))
+    known, hidden_parts = [], []
+    for call, size in zip(calls, (cut, rows - cut)):
+        some, part = run_nets(
+            row_at, [p for p, _ in call], [q for _, q in call], *exchanged[0],
+            [head[3], head[2]], size, row_count, (), (1, 0),
         )
-        for i, n in enumerate(group):
-            hidden[n], parts[n] = got_hidden[i].reshape(tokens, units), got_parts[i]
-
-    piece = tokens // peers
-    known = jnp.concatenate([parts[3], parts[2][:, :1]], axis=1)
-    known = known.transpose(1, 0, 2).reshape(acts + 1, peers, piece).transpose(1, 0, 2)
+        known.append(part)
+        hidden_parts.append(some)
+    critics, late = run_nets(
+        row_at, pieces, places, *exchanged[1], head[:2], rows, row_count,
+        (own_actions, act_w), (0, 1),
+    )
+
+    group = 32 // col_count
+    known = jnp.concatenate(known, axis=2).reshape(peers, group, rows)
     known = lax.all_to_all(known, ("row", "col"), 0, 0, tiled=True)
     known = jnp.sum(known, axis=0)
-    known = jnp.concatenate([known, swap(known[acts:], "dp", 1)], axis=0)
+    at = acts % group
+    other = swap(known[at : at + 1], "dp", 1)
+    spot = (lax.broadcasted_iota(jnp.int32, known.shape, 0) == at + 1) & (col_at == acts // group)
+    known = jnp.where(spot, other, known)
     known = spread(known, ("row", "col"))
-    known = known.transpose(1, 0, 2).reshape(acts + 2, tokens)
-
-    late = jnp.concatenate([parts[n][:, 0].reshape(1, tokens) for n in (0, 1)], axis=0)
+    known = known.reshape(row_count, 32, rows).transpose(1, 0, 2).reshape(32, tokens)
+
     for axis, size in (("col", col_count), ("row", row_count)):
         late = sum((swap(late, axis, k) for k in range(1, size)), late)
     late = jnp.concatenate([late, swap(late, "dp", 1)], axis=0)
 
     vmem = pl.BlockSpec(memory_space=pltpu.VMEM)
     smem = pl.BlockSpec(memory_space=pltpu.SMEM)
+    hidden = [h.reshape(tokens, units) for h in critics]
+    hidden += [hidden_parts[i][n] for n in (1, 0) for i in (0, 1)]
     adv, last = pl.pallas_call(
         functools.partial(tail_kernel, acts=acts),
         out_shape=(
             jax.ShapeDtypeStruct((1, tokens), F32),
             jax.ShapeDtypeStruct((dp_count * peers, acts + 5, units), BF16),
         ),
-        in_specs=[smem] + [vmem] * 8,
+        in_specs=[smem] + [vmem] * 4 + [pl.BlockSpec(memory_space=pl.ANY)] * 6,
         out_specs=(vmem, vmem),
-        scratch_shapes=[pltpu.VMEM((acts + 5, units), F32)],
+        scratch_shapes=[
+            pltpu.VMEM((acts + 5, units), F32),
+            *[pltpu.VMEM(h.shape, BF16) for h in hidden],
+            pltpu.SemaphoreType.DMA((len(hidden),)),
+        ],
         compiler_params=pltpu.CompilerParams(vmem_limit_bytes=24 * 1024 * 1024),
     )(
         dp_at.reshape(1), late, pack, known, policy_scale[:, None],
-        hidden[0], hidden[1], hidden[2], hidden[3],
+        *hidden,
     )
     advantage = lax.dynamic_slice_in_dim(adv[0], row_at * rows, rows, 0)
     last = lax.all_to_all(last, ("dp", "row", "col"), 0, 0, tiled=True)

time: 359 us -> 373 us (1.039)
  waiting for transfers between devices: 197 us -> 215 us
  local copies, waits for them, and re-layouts: 62.6 us -> 46.7 us
  Pallas kernels: 22.2 us -> 26.8 us
    unnamed x118 -> x136, local copies, waits for them, and re-layouts: 43.6 us -> 28.2 us
    ppermute x0 -> x4, starting transfers between devices: none -> 9.02 us  [the longest x2 6.87 us: shards(): far = lax.ppermute(sent, 'col', far)]
    ppermute x0 -> x4, waiting for transfers between devices: none -> 9.02 us  [the longest x2 9.01 us: shards(): far = lax.ppermute(sent, 'col', far)]
    ppermute x41 -> x39, starting transfers between devices: 55.2 us -> 49.8 us  [swap(): return lax.ppermute(x, axis, [(i, i ^ bit) for i in range(size)])]
    all_to_all x2, waiting for transfers between devices: 25.9 us -> 31 us  [spread(): return lax.all_to_all(x, axes, 0, 0, tiled=True)]
    ppermute x41 -> x39, waiting for transfers between devices: 155 us -> 159 us  [swap(): return lax.ppermute(x, axis, [(i, i ^ bit) for i in range(size)])]
    pallas_call x2 -> x3, Pallas kernels: 20.5 us -> 23.7 us  [run_nets(): pl.pallas_call(functools.partial(net_kernel, places=places, row_count=row...]
  transfers between devices with their start and end apart: 45 -> 47, of which waited for: 23 -> 19; matrix products, arithmetic and copies ran while one was open for 7% -> 7% of each run, Pallas kernels for 6% -> 6%
where the time goes in v2:
time: 373 us; the launch traced here: 371 us
  waiting for transfers between devices  215 us (58%)
  starting transfers between devices  73.5 us (20%)
  local copies, waits for them, and re-layouts  46.7 us (13%)
  Pallas kernels  26.8 us (7%)
  other arithmetic  7.7 us (2%)
    ppermute x39, waiting for transfers between devices, swap(): return lax.ppermute(x, axis, [(i, i ^ bit) for i in range(size)])  159 us
    ppermute x39, starting transfers between devices, swap(): return lax.ppermute(x, axis, [(i, i ^ bit) for i in range(size)])  49.8 us
    all_to_all x2, waiting for transfers between devices, spread(): return lax.all_to_all(x, axes, 0, 0, tiled=True)  31 us
    unnamed x136, local copies, waits for them, and re-layouts  28.2 us
    pallas_call x3, Pallas kernels, run_nets(): pl.pallas_call(functools.partial(net_kernel, places=places, row_count=row...  23.7 us
    all_to_all x1, waiting for transfers between devices, shards(): last = lax.all_to_all(last, ('dp', 'row', 'col'), 0, 0, tiled=True)  15.7 us
    ppermute x2, waiting for transfers between devices, shards(): far = lax.ppermute(sent, 'col', far)  9.01 us
    dynamic_slice x1, local copies, waits for them, and re-layouts, shards(): lax.dynamic_slice_in_dim(mine, jnp.bitwise_xor(col_at, k) * units, units, 2)  8.5 us
  transfers between devices with their start and end apart: 47, of which 19 were waited for; matrix products, arithmetic and copies ran while one was open for 7% of the time, Pallas kernels for 6%

profile of v2, /device:TPU:0, one launch (start us, length us, event | category | flops | bytes accessed | tf_op | source)
XLA Modules:
  0.0 371.2 jit_solution(2649841367990822804)
XLA Ops:
  2.7 4.1 %collective-permute-start = (bf16[2,32,512]{2,1,0:T(8,128)(2,1)S(1)}, bf16[2,32,512]{2,1,0:T(8,128)(2,1)S(1)}, u32[]{:S(2)}, u32[]{:S(2)}) collective-permute-start(bf16[2,32,512]{2,1,0:T(8,128)(2,1)S(1)} %get-tuple-element.34), channel_id=1, source_target_pairs={{0,2},{1,3},{2,0},{3,1},{4,6},{5,7},{6,4},{7,5},{8,10},{9,11},{10,... | collective-permute-start | bytes 196616 | tf_op jit(solution)/shard_map/ppermute | solution.py:21
  6.8 8.5 %constant_dynamic-slice_fusion.9 = (bf16[2,512,256]{2,1,0:T(8,128)(2,1)}, bf16[2,512,256]{2,1,0:T(8,128)(2,1)}, bf16[2,512,256]{2,1,0:T(8,128)(2,1)S(1)}, bf16[2...) fusion(bf16[4,1024,1024]{2,1,0:T(8,128)(2,1)} %param.14, ...), kind=kLoop, calls=%fused_computation.39 | loop fusion | bytes 8388628 | tf_op jit(solution)/shard_map/dynamic_slice | solution.py:287
  16.8 3.5 collective-permute-start.20
  23.5 23.9 %collective-permute-done.20 = bf16[2,32,512]{2,1,0:T(8,128)(2,1)S(1)} collective-permute-done((bf16[2,32,512]{2,1,0:T(8,128)(2,1)S(1)}, bf16[2,32,512]{2,1,0:T(8,128)(2,1)S(1)}, u32[]{:S(2)}, u32[]{:S(2)}) %collective-permute-start.20) | collective-permute-done | bytes 65568 | tf_op jit(solution)/shard_map/ppermute | solution.py:21
  47.6 16.0 %collective-permute-done.21 = bf16[2,32,1024]{2,1,0:T(8,128)(2,1)S(1)} collective-permute-done((bf16[2,32,1024]{2,1,0:T(8,128)(2,1)S(1)}, bf16[2,32,1024]{2,1,0:T(8,128)(2,1)S(1)}, u32[]{:S(2)}, u32[]{:S(2)}) %collective-permute-start.21) | collective-permute-done | bytes 131104 | tf_op jit(solution)/shard_map/ppermute | solution.py:21
  67.9 2.3 collective-permute-done.2.refs_1_
  70.2 1.9 collective-permute-start.40
  74.3 5.0 %collective-permute-start.28 = (bf16[2,512,256]{2,1,0:T(8,128)(2,1)S(1)}, bf16[2,512,256]{2,1,0:T(8,128)(2,1)S(1)}, u32[]{:S(2)}, u32[]{:S(2)}) collective-permute-start(bf16[2,512,256]{2,1,0:T(8,128)(2,1)S(1)} %get-tuple-element.27), channel_id=1, source_target_pairs={{0,3},{3,0},{4,7},{7,4},{8,11},{11,8},{12,15},{15,12},{16,19},{19,... | collective-permute-start | bytes 1572872 | tf_op jit(solution)/shard_map/ppermute | solution.py:293
  80.1 9.0 %collective-permute-done.40 = bf16[2,512,256]{2,1,0:T(8,128)(2,1)} collective-permute-done((bf16[2,512,256]{2,1,0:T(8,128)(2,1)}, bf16[2,512,256]{2,1,0:T(8,128)(2,1)}, u32[]{:S(2)}, u32[]{:S(2)}) %collective-permute-start.40) | collective-permute-done | bytes 524320 | tf_op jit(solution)/shard_map/ppermute | solution.py:293
  89.1 32.7 %collective-permute-done.37 = bf16[2,512,256]{2,1,0:T(8,128)(2,1)} collective-permute-done((bf16[2,512,256]{2,1,0:T(8,128)(2,1)}, bf16[2,512,256]{2,1,0:T(8,128)(2,1)}, u32[]{:S(2)}, u32[]{:S(2)}) %collective-permute-start.37) | collective-permute-done | bytes 524320 | tf_op jit(solution)/shard_map/ppermute | solution.py:21
  122.9 2.1 collective-permute-start.26
  125.0 14.1 %collective-permute-start.6 = (bf16[2,96,1024]{2,1,0:T(8,128)(2,1)S(1)}, bf16[2,96,1024]{2,1,0:T(8,128)(2,1)S(1)}, u32[]{:S(2)}, u32[]{:S(2)}) collective-permute-start(bf16[2,96,1024]{2,1,0:T(8,128)(2,1)S(1)} %pad_maximum_fusion.6), channel_id=1, source_target_pairs={{0,1},{1,0},{2,3},{3,2},{4,5},{5,4},{6,7},{7,6},{8,9},{9,8},{10,11... | collective-permute-start | bytes 1179656 | tf_op jit(solution)/shard_map/ppermute | solution.py:21
  140.7 9.1 %collective-permute-done.25 = bf16[2,512,256]{2,1,0:T(8,128)(2,1)S(1)} collective-permute-done((bf16[2,512,256]{2,1,0:T(8,128)(2,1)}, bf16[2,512,256]{2,1,0:T(8,128)(2,1)S(1)}, u32[]{:S(2)}, u32[]{:S(2)}) %collective-permute-start.25) | collective-permute-done | bytes 524320 | tf_op jit(solution)/shard_map/ppermute | solution.py:21
  150.3 14.4 %collective-permute-done.6 = bf16[2,96,1024]{2,1,0:T(8,128)(2,1)S(1)} collective-permute-done((bf16[2,96,1024]{2,1,0:T(8,128)(2,1)S(1)}, bf16[2,96,1024]{2,1,0:T(8,128)(2,1)S(1)}, u32[]{:S(2)}, u32[]{:S(2)}) %collective-permute-start.6) | collective-permute-done | bytes 393248 | tf_op jit(solution)/shard_map/ppermute | solution.py:21
  166.9 8.0 %collective-permute-done.11 = bf16[2,128,1024]{2,1,0:T(8,128)(2,1)S(1)} collective-permute-done((bf16[2,128,1024]{2,1,0:T(8,128)(2,1)S(1)}, bf16[2,128,1024]{2,1,0:T(8,128)(2,1)S(1)}, u32[]{:S(2)}, u32[]{:S(2)}) %collective-permute-start.11) | collective-permute-done | bytes 524320 | tf_op jit(solution)/shard_map/ppermute | solution.py:21
  177.8 12.9 %collective-permute-done.24.refs_19_.refs_7_ = bf16[2,32,2048]{2,1,0:T(8,128)(2,1)S(1)} collective-permute-done((bf16[2,32,2048]{2,1,0:T(8,128)(2,1)S(1)}, bf16[2,32,2048]{2,1,0:T(8,128)(2,1)S(1)}, u32[]{:S(2)}, u32[]{:S(2)}) %collective-permute-start.24) | collective-permute-done | bytes 262176 | tf_op jit(solution)/shard_map/ppermute | solution.py:21
  194.4 10.2 %collective-permute-done.8.refs_6_ = bf16[2,96,2048]{2,1,0:T(8,128)(2,1)S(1)} collective-permute-done((bf16[2,96,2048]{2,1,0:T(8,128)(2,1)S(1)}, bf16[2,96,2048]{2,1,0:T(8,128)(2,1)S(1)}, u32[]{:S(2)}, u32[]{:S(2)}) %collective-permute-start.8) | collective-permute-done | bytes 786464 | tf_op jit(solution)/shard_map/ppermute | solution.py:21
  204.6 15.7 %collective-permute-done.17.refs_13_.refs_1_ = bf16[2,96,2048]{2,1,0:T(8,128)(2,1)S(1)} collective-permute-done((bf16[2,96,2048]{2,1,0:T(8,128)(2,1)S(1)}, bf16[2,96,2048]{2,1,0:T(8,128)(2,1)S(1)}, u32[]{:S(2)}, u32[]{:S(2)}) %collective-permute-start.17) | collective-permute-done | bytes 786464 | tf_op jit(solution)/shard_map/ppermute | solution.py:21
  224.0 4.2 %all-to-all-start = ((f32[4,27,384]{2,1,0:T(8,128)}), f32[4,27,384]{2,1,0:T(8,128)}, u32[]{:S(2)}, u32[]{:S(2)}) async-start(f32[4,27,384]{2,1,0:T(8,128)} %broadcast_in_dim.36), calls=%async_computation | async-start | bytes 393216 | tf_op jit(solution)/shard_map/all_to_all | solution.py:27
  228.2 8.1 %collective-permute-done.19.refs_15_.refs_3_ = bf16[2,96,2048]{2,1,0:T(8,128)(2,1)} collective-permute-done((bf16[2,96,2048]{2,1,0:T(8,128)(2,1)}, bf16[2,96,2048]{2,1,0:T(8,128)(2,1)}, u32[]{:S(2)}, u32[]{:S(2)}) %collective-permute-start.19) | collective-permute-done | bytes 786464 | tf_op jit(solution)/shard_map/ppermute | solution.py:21
  242.9 24.2 %all-to-all-done = f32[4,27,384]{2,1,0:T(8,128)} async-done(((f32[4,27,384]{2,1,0:T(8,128)}), f32[4,27,384]{2,1,0:T(8,128)}, u32[]{:S(2)}, u32[]{:S(2)}) %all-to-all-start) | async-done | bytes 165920 | tf_op jit(solution)/shard_map/all_to_all | solution.py:27
  274.5 5.2 %shard_map.114 = (bf16[4,128,256]{2,1,0:T(8,128)(2,1)S(1)}, bf16[4,128,256]{2,1,0:T(8,128)(2,1)S(1)}, f32[4,32,128]{2,1,0:T(8,128)S(1)}) custom-call(s32[1]{0:T(128)} %bitcast.1.row_ref, bf16[2,96,2048]{2,1,0:T(8,128)(2,1)S(1)} %pad_maximum_fusion.4.refs_12_.refs_0_, bf16[2,96,2048]{2,1,0:T(8,128)(2,1)S(1)} %copy-done.2, ...), custom_call_target="tpu_custom_call" | custom-call | flops 2147483648 | bytes 4194304 | tf_op jit(solution)/shard_map/pallas_call | solution.py:101
  281.2 7.7 %shard_map.113 = (bf16[4,256,256]{2,1,0:T(8,128)(2,1)S(1)}, bf16[4,256,256]{2,1,0:T(8,128)(2,1)S(1)}, f32[4,32,256]{2,1,0:T(8,128)S(1)}) custom-call(s32[1]{0:T(128)} %bitcast.1.row_ref, bf16[2,32,2048]{2,1,0:T(8,128)(2,1)S(1)} %copy-done.27, bf16[2,32,2048]{2,1,0:T(8,128)(2,1)S(1)} %copy-done.37, bf16[2,32,2048]{2,1,0:T(8,128)(2,1)S(1)} %copy-done.40, ...), custom_call_target="tpu_custom_call" | custom-call | flops 4294967296 | bytes 8388608 | tf_op jit(solution)/shard_map/pallas_call | solution.py:101
  291.2 3.7 %all-to-all-start.1 = ((f32[16,8,384]{2,1,0:T(8,128)}), f32[16,8,384]{2,1,0:T(8,128)S(1)}, u32[]{:S(2)}, u32[]{:S(2)}) async-start(f32[16,8,384]{2,1,0:T(8,128)} %bitcast.8), calls=%async_computation.1 | async-start | bytes 393216 | tf_op jit(solution)/shard_map/all_to_all | solution.py:315
  308.1 10.9 %shard_map.112 = (bf16[4,384,256]{2,1,0:T(8,128)(2,1)S(1)}, bf16[4,384,256]{2,1,0:T(8,128)(2,1)S(1)}, f32[2,1536]{1,0:T(2,128)S(1)}) custom-call(s32[1]{0:T(128)} %bitcast.1.row_ref, bf16[2,32,2048]{2,1,0:T(8,128)(2,1)S(1)} %copy-done.28, bf16[2,32,2048]{2,1,0:T(8,128)(2,1)S(1)} %copy-done.38, bf16[2,32,2048]{2,1,0:T(8,128)(2,1)S(1)} %copy-done.41, ...), custom_call_target="tpu_custom_call" | custom-call | flops 6442450944 | bytes 12582912 | tf_op jit(solution)/shard_map/pallas_call | solution.py:101
  320.7 2.4 collective-permute-start.31
  325.3 3.3 collective-permute-done.32
  332.9 4.2 %all-to-all-start.2 = ((f32[16,8,384]{2,1,0:T(8,128)}), f32[16,8,384]{2,1,0:T(8,128)}, u32[]{:S(2)}, u32[]{:S(2)}) async-start(f32[16,8,384]{2,1,0:T(8,128)} %broadcast_in_dim.38), calls=%async_computation.2 | async-start | bytes 393216 | tf_op jit(solution)/shard_map/all_to_all | solution.py:27
  338.4 6.7 %all-to-all-done.2 = f32[16,8,384]{2,1,0:T(8,128)} async-done(((f32[16,8,384]{2,1,0:T(8,128)}), f32[16,8,384]{2,1,0:T(8,128)}, u32[]{:S(2)}, u32[]{:S(2)}) %all-to-all-start.2) | async-done | bytes 196640 | tf_op jit(solution)/shard_map/all_to_all | solution.py:27
  347.1 3.1 shard_map.115
  350.2 2.6 all-to-all-start.3
  353.4 15.7 %all-to-all-done.3 = bf16[32,29,256]{2,1,0:T(8,128)(2,1)S(1)} async-done(((bf16[32,29,256]{2,1,0:T(8,128)(2,1)}), bf16[32,29,256]{2,1,0:T(8,128)(2,1)S(1)}, u32[]{:S(2)}, u32[]{:S(2)}) %all-to-all-start.3) | async-done | bytes 475168 | tf_op jit(solution)/shard_map/all_to_all | solution.py:351
  (256 shorter events, 74.2 us)
Async XLA Ops:
  15.3 64.0 %collective-permute-start.39 = (bf16[2,512,256]{2,1,0:T(8,128)(2,1)}, bf16[2,512,256]{2,1,0:T(8,128)(2,1)}, u32[]{:S(2)}, u32[]{:S(2)}) collective-permute-start(bf16[2,512,256]{2,1,0:T(8,128)(2,1)} %get-tuple-element.31), channel_id=1, source_target_pairs={{1,2},{2,1},{5,6},{6,5},{9,10},{10,9},{13,14},{14,13},{17,18},{18,... | collective-permute-start | bytes 1572872 | tf_op jit(solution)/shard_map/ppermute | solution.py:292
  16.8 30.7 %collective-permute-start.20 = (bf16[2,32,512]{2,1,0:T(8,128)(2,1)S(1)}, bf16[2,32,512]{2,1,0:T(8,128)(2,1)S(1)}, u32[]{:S(2)}, u32[]{:S(2)}) collective-permute-start(bf16[2,32,512]{2,1,0:T(8,128)(2,1)S(1)} %get-tuple-element.33), channel_id=1, source_target_pairs={{0,2},{1,3},{2,0},{3,1},{4,6},{5,7},{6,4},{7,5},{8,10},{9,11},{10,... | collective-permute-start | bytes 196616 | tf_op jit(solution)/shard_map/ppermute | solution.py:21
  20.3 27.2 %collective-permute-start.1 = (bf16[2,32,1024]{2,1,0:T(8,128)(2,1)S(1)}, bf16[2,32,1024]{2,1,0:T(8,128)(2,1)S(1)}, u32[]{:S(2)}, u32[]{:S(2)}) collective-permute-start(bf16[2,32,1024]{2,1,0:T(8,128)(2,1)S(1)} %pad_maximum_fusion.11), channel_id=1, source_target_pairs={{0,1},{1,0},{2,3},{3,2},{4,5},{5,4},{6,7},{7,6},{8,9},{9,8},{10,11... | collective-permute-start | bytes 393224 | tf_op jit(solution)/shard_map/ppermute | solution.py:21
  20.5 44.7 %collective-permute-start.5 = (bf16[2,96,512]{2,1,0:T(8,128)(2,1)S(1)}, bf16[2,96,512]{2,1,0:T(8,128)(2,1)S(1)}, u32[]{:S(2)}, u32[]{:S(2)}) collective-permute-start(bf16[2,96,512]{2,1,0:T(8,128)(2,1)S(1)} %get-tuple-element.36), channel_id=1, source_target_pairs={{0,2},{1,3},{2,0},{3,1},{4,6},{5,7},{6,4},{7,5},{8,10},{9,11},{10,... | collective-permute-start | bytes 589832 | tf_op jit(solution)/shard_map/ppermute | solution.py:21
  22.0 45.3 %collective-permute-start.10 = (bf16[2,128,512]{2,1,0:T(8,128)(2,1)S(1)}, bf16[2,128,512]{2,1,0:T(8,128)(2,1)S(1)}, u32[]{:S(2)}, u32[]{:S(2)}) collective-permute-start(bf16[2,128,512]{2,1,0:T(8,128)(2,1)S(1)} %slice.60), channel_id=1, source_target_pairs={{0,2},{1,3},{2,0},{3,1},{4,6},{5,7},{6,4},{7,5},{8,10},{9,11},{10,... | collective-permute-start | bytes 786440 | tf_op jit(solution)/shard_map/ppermute | solution.py:21
  47.5 19.2 %collective-permute-start.15 = (bf16[2,96,512]{2,1,0:T(8,128)(2,1)S(1)}, bf16[2,96,512]{2,1,0:T(8,128)(2,1)S(1)}, u32[]{:S(2)}, u32[]{:S(2)}) collective-permute-start(bf16[2,96,512]{2,1,0:T(8,128)(2,1)S(1)} %get-tuple-element.35), channel_id=1, source_target_pairs={{0,2},{1,3},{2,0},{3,1},{4,6},{5,7},{6,4},{7,5},{8,10},{9,11},{10,... | collective-permute-start | bytes 589832 | tf_op jit(solution)/shard_map/ppermute | solution.py:21
  70.2 18.9 %collective-permute-start.40 = (bf16[2,512,256]{2,1,0:T(8,128)(2,1)}, bf16[2,512,256]{2,1,0:T(8,128)(2,1)}, u32[]{:S(2)}, u32[]{:S(2)}) collective-permute-start(bf16[2,512,256]{2,1,0:T(8,128)(2,1)} %get-tuple-element.31), channel_id=1, source_target_pairs={{0,3},{3,0},{4,7},{7,4},{8,11},{11,8},{12,15},{15,12},{16,19},{19,... | collective-permute-start | bytes 1572872 | tf_op jit(solution)/shard_map/ppermute | solution.py:293
  72.8 49.0 %collective-permute-start.37 = (bf16[2,512,256]{2,1,0:T(8,128)(2,1)}, bf16[2,512,256]{2,1,0:T(8,128)(2,1)}, u32[]{:S(2)}, u32[]{:S(2)}) collective-permute-start(bf16[2,512,256]{2,1,0:T(8,128)(2,1)} %get-tuple-element.26), channel_id=1, source_target_pairs={{0,2},{1,3},{2,0},{3,1},{4,6},{5,7},{6,4},{7,5},{8,10},{9,11},{10,... | collective-permute-start | bytes 1572872 | tf_op jit(solution)/shard_map/ppermute | solution.py:21
  73.1 51.9 %collective-permute-start.27 = (bf16[2,512,256]{2,1,0:T(8,128)(2,1)S(1)}, bf16[2,512,256]{2,1,0:T(8,128)(2,1)S(1)}, u32[]{:S(2)}, u32[]{:S(2)}) collective-permute-start(bf16[2,512,256]{2,1,0:T(8,128)(2,1)S(1)} %get-tuple-element.27), channel_id=1, source_target_pairs={{1,2},{2,1},{5,6},{6,5},{9,10},{10,9},{13,14},{14,13},{17,18},{18,... | collective-permute-start | bytes 1572872 | tf_op jit(solution)/shard_map/ppermute | solution.py:292
  74.3 64.8 %collective-permute-start.28 = (bf16[2,512,256]{2,1,0:T(8,128)(2,1)S(1)}, bf16[2,512,256]{2,1,0:T(8,128)(2,1)S(1)}, u32[]{:S(2)}, u32[]{:S(2)}) collective-permute-start(bf16[2,512,256]{2,1,0:T(8,128)(2,1)S(1)} %get-tuple-element.27), channel_id=1, source_target_pairs={{0,3},{3,0},{4,7},{7,4},{8,11},{11,8},{12,15},{15,12},{16,19},{19,... | collective-permute-start | bytes 1572872 | tf_op jit(solution)/shard_map/ppermute | solution.py:293
  79.3 43.6 %collective-permute-start.38 = (bf16[2,512,256]{2,1,0:T(8,128)(2,1)}, bf16[2,512,256]{2,1,0:T(8,128)(2,1)S(1)}, u32[]{:S(2)}, u32[]{:S(2)}) collective-permute-start(bf16[2,512,256]{2,1,0:T(8,128)(2,1)} %get-tuple-element.32), channel_id=1, source_target_pairs={{0,1},{1,0},{2,3},{3,2},{4,5},{5,4},{6,7},{7,6},{8,9},{9,8},{10,11... | collective-permute-start | bytes 1572872 | tf_op jit(solution)/shard_map/ppermute | solution.py:21
  89.1 60.6 %collective-permute-start.25 = (bf16[2,512,256]{2,1,0:T(8,128)(2,1)}, bf16[2,512,256]{2,1,0:T(8,128)(2,1)S(1)}, u32[]{:S(2)}, u32[]{:S(2)}) collective-permute-start(bf16[2,512,256]{2,1,0:T(8,128)(2,1)} %get-tuple-element.29), channel_id=1, source_target_pairs={{0,2},{1,3},{2,0},{3,1},{4,6},{5,7},{6,4},{7,5},{8,10},{9,11},{10,... | collective-permute-start | bytes 1572872 | tf_op jit(solution)/shard_map/ppermute | solution.py:21
  121.8 18.7 %collective-permute-start.16 = (bf16[2,96,1024]{2,1,0:T(8,128)(2,1)S(1)}, bf16[2,96,1024]{2,1,0:T(8,128)(2,1)S(1)}, u32[]{:S(2)}, u32[]{:S(2)}) collective-permute-start(bf16[2,96,1024]{2,1,0:T(8,128)(2,1)S(1)} %pad_maximum_fusion.7), channel_id=1, source_target_pairs={{0,1},{1,0},{2,3},{3,2},{4,5},{5,4},{6,7},{7,6},{8,9},{9,8},{10,11... | collective-permute-start | bytes 1179656 | tf_op jit(solution)/shard_map/ppermute | solution.py:21
  122.9 42.3 %collective-permute-start.26 = (bf16[2,512,256]{2,1,0:T(8,128)(2,1)}, bf16[2,512,256]{2,1,0:T(8,128)(2,1)S(1)}, u32[]{:S(2)}, u32[]{:S(2)}) collective-permute-start(bf16[2,512,256]{2,1,0:T(8,128)(2,1)} %get-tuple-element.28), channel_id=1, source_target_pairs={{0,1},{1,0},{2,3},{3,2},{4,5},{5,4},{6,7},{7,6},{8,9},{9,8},{10,11... | collective-permute-start | bytes 1572872 | tf_op jit(solution)/shard_map/ppermute | solution.py:21
  125.0 39.6 %collective-permute-start.6 = (bf16[2,96,1024]{2,1,0:T(8,128)(2,1)S(1)}, bf16[2,96,1024]{2,1,0:T(8,128)(2,1)S(1)}, u32[]{:S(2)}, u32[]{:S(2)}) collective-permute-start(bf16[2,96,1024]{2,1,0:T(8,128)(2,1)S(1)} %pad_maximum_fusion.6), channel_id=1, source_target_pairs={{0,1},{1,0},{2,3},{3,2},{4,5},{5,4},{6,7},{7,6},{8,9},{9,8},{10,11... | collective-permute-start | bytes 1179656 | tf_op jit(solution)/shard_map/ppermute | solution.py:21
  139.1 35.8 %collective-permute-start.11 = (bf16[2,128,1024]{2,1,0:T(8,128)(2,1)S(1)}, bf16[2,128,1024]{2,1,0:T(8,128)(2,1)S(1)}, u32[]{:S(2)}, u32[]{:S(2)}) collective-permute-start(bf16[2,128,1024]{2,1,0:T(8,128)(2,1)S(1)} %pad_maximum_fusion.5), channel_id=1, source_target_pairs={{0,1},{1,0},{2,3},{3,2},{4,5},{5,4},{6,7},{7,6},{8,9},{9,8},{10,11... | collective-permute-start | bytes 1572872 | tf_op jit(solution)/shard_map/ppermute | solution.py:21
  140.5 96.4 %collective-permute-start.41 = (bf16[2,2048,256]{2,1,0:T(8,128)(2,1)S(1)}, bf16[2,2048,256]{2,1,0:T(8,128)(2,1)}, u32[]{:S(2)}, u32[]{:S(2)}) collective-permute-start(bf16[2,2048,256]{2,1,0:T(8,128)(2,1)S(1)} %pad_maximum_fusion.1.refs_12_.refs_8_), channel_id=1, source_target_pairs={{0,16},{16,0},{1,17},{17,1},{2,18},{18,2},{3,19},{19,3},{4,20},{20... | collective-permute-start | bytes 6291464 | tf_op jit(solution)/shard_map/ppermute | solution.py:21
  149.8 26.7 %collective-permute-start.4 = (bf16[2,32,2048]{2,1,0:T(8,128)(2,1)S(1)}, bf16[2,32,2048]{2,1,0:T(8,128)(2,1)S(1)}, u32[]{:S(2)}, u32[]{:S(2)}) collective-permute-start(bf16[2,32,2048]{2,1,0:T(8,128)(2,1)S(1)} %copy-done.36), channel_id=1, source_target_pairs={{0,8},{4,12},{8,0},{12,4},{1,9},{5,13},{9,1},{13,5},{2,10},{6,14},... | collective-permute-start | bytes 786440 | tf_op jit(solution)/shard_map/ppermute | solution.py:21
  164.7 26.6 %collective-permute-start.18 = (bf16[2,96,2048]{2,1,0:T(8,128)(2,1)S(1)}, bf16[2,96,2048]{2,1,0:T(8,128)(2,1)}, u32[]{:S(2)}, u32[]{:S(2)}) collective-permute-start(bf16[2,96,2048]{2,1,0:T(8,128)(2,1)S(1)} %pad_maximum_fusion.4.refs_12_.refs_0_), channel_id=1, source_target_pairs={{0,8},{4,12},{8,0},{12,4},{1,9},{5,13},{9,1},{13,5},{2,10},{6,14},... | collective-permute-start | bytes 2359304 | tf_op jit(solution)/shard_map/ppermute | solution.py:21
  165.3 25.4 %collective-permute-start.24 = (bf16[2,32,2048]{2,1,0:T(8,128)(2,1)S(1)}, bf16[2,32,2048]{2,1,0:T(8,128)(2,1)S(1)}, u32[]{:S(2)}, u32[]{:S(2)}) collective-permute-start(bf16[2,32,2048]{2,1,0:T(8,128)(2,1)S(1)} %copy-done.13), channel_id=1, source_target_pairs={{0,8},{4,12},{8,0},{12,4},{1,9},{5,13},{9,1},{13,5},{2,10},{6,14},... | collective-permute-start | bytes 786440 | tf_op jit(solution)/shard_map/ppermute | solution.py:21
  174.9 29.7 %collective-permute-start.8 = (bf16[2,96,2048]{2,1,0:T(8,128)(2,1)S(1)}, bf16[2,96,2048]{2,1,0:T(8,128)(2,1)S(1)}, u32[]{:S(2)}, u32[]{:S(2)}) collective-permute-start(bf16[2,96,2048]{2,1,0:T(8,128)(2,1)S(1)} %pad_maximum_fusion.3.refs_4_), channel_id=1, source_target_pairs={{0,8},{4,12},{8,0},{12,4},{1,9},{5,13},{9,1},{13,5},{2,10},{6,14},... | collective-permute-start | bytes 2359304 | tf_op jit(solution)/shard_map/ppermute | solution.py:21
  177.2 45.5 %collective-permute-start.12 = (bf16[2,128,2048]{2,1,0:T(8,128)(2,1)}, bf16[2,128,2048]{2,1,0:T(8,128)(2,1)}, u32[]{:S(2)}, u32[]{:S(2)}) collective-permute-start(bf16[2,128,2048]{2,1,0:T(8,128)(2,1)} %pad_maximum_fusion.2.refs_8_), channel_id=1, source_target_pairs={{0,4},{4,0},{8,12},{12,8},{1,5},{5,1},{9,13},{13,9},{2,6},{6,2},{1... | collective-permute-start | bytes 3145736 | tf_op jit(solution)/shard_map/ppermute | solution.py:21
  190.7 29.6 %collective-permute-start.17 = (bf16[2,96,2048]{2,1,0:T(8,128)(2,1)S(1)}, bf16[2,96,2048]{2,1,0:T(8,128)(2,1)S(1)}, u32[]{:S(2)}, u32[]{:S(2)}) collective-permute-start(bf16[2,96,2048]{2,1,0:T(8,128)(2,1)S(1)} %pad_maximum_fusion.4.refs_12_.refs_0_), channel_id=1, source_target_pairs={{0,4},{4,0},{8,12},{12,8},{1,5},{5,1},{9,13},{13,9},{2,6},{6,2},{1... | collective-permute-start | bytes 2359304 | tf_op jit(solution)/shard_map/ppermute | solution.py:21
  191.4 44.9 %collective-permute-start.19 = (bf16[2,96,2048]{2,1,0:T(8,128)(2,1)}, bf16[2,96,2048]{2,1,0:T(8,128)(2,1)}, u32[]{:S(2)}, u32[]{:S(2)}) collective-permute-start(bf16[2,96,2048]{2,1,0:T(8,128)(2,1)} %collective-permute-done.18.refs_14_.refs_2_), channel_id=1, source_target_pairs={{0,4},{4,0},{8,12},{12,8},{1,5},{5,1},{9,13},{13,9},{2,6},{6,2},{1... | collective-permute-start | bytes 2359304 | tf_op jit(solution)/shard_map/ppermute | solution.py:21
  204.6 90.3 %collective-permute-start.29 = (bf16[2,2048,256]{2,1,0:T(8,128)(2,1)}, bf16[2,2048,256]{2,1,0:T(8,128)(2,1)}, u32[]{:S(2)}, u32[]{:S(2)}) collective-permute-start(bf16[2,2048,256]{2,1,0:T(8,128)(2,1)} %pad_maximum_fusion.refs_20_), channel_id=1, source_target_pairs={{0,16},{16,0},{1,17},{17,1},{2,18},{18,2},{3,19},{19,3},{4,20},{20... | collective-permute-start | bytes 6291464 | tf_op jit(solution)/shard_map/ppermute | solution.py:21
  221.2 59.9 %collective-permute-start.13 = (bf16[2,128,2048]{2,1,0:T(8,128)(2,1)}, bf16[2,128,2048]{2,1,0:T(8,128)(2,1)}, u32[]{:S(2)}, u32[]{:S(2)}) collective-permute-start(bf16[2,128,2048]{2,1,0:T(8,128)(2,1)} %pad_maximum_fusion.2.refs_8_), channel_id=1, source_target_pairs={{0,8},{4,12},{8,0},{12,4},{1,9},{5,13},{9,1},{13,5},{2,10},{6,14},... | collective-permute-start | bytes 3145736 | tf_op jit(solution)/shard_map/ppermute | solution.py:21
  222.7 58.4 %collective-permute-start.14 = (bf16[2,128,2048]{2,1,0:T(8,128)(2,1)}, bf16[2,128,2048]{2,1,0:T(8,128)(2,1)}, u32[]{:S(2)}, u32[]{:S(2)}) collective-permute-start(bf16[2,128,2048]{2,1,0:T(8,128)(2,1)} %collective-permute-done.12.refs_9_), channel_id=1, source_target_pairs={{0,8},{4,12},{8,0},{12,4},{1,9},{5,13},{9,1},{13,5},{2,10},{6,14},... | collective-permute-start | bytes 3145736 | tf_op jit(solution)/shard_map/ppermute | solution.py:21
  224.0 43.1 %all-to-all-start = ((f32[4,27,384]{2,1,0:T(8,128)}), f32[4,27,384]{2,1,0:T(8,128)}, u32[]{:S(2)}, u32[]{:S(2)}) async-start(f32[4,27,384]{2,1,0:T(8,128)} %broadcast_in_dim.36), calls=%async_computation | async-start | bytes 393216 | tf_op jit(solution)/shard_map/all_to_all | solution.py:27
  236.4 44.7 %collective-permute-start.7 = (bf16[2,96,2048]{2,1,0:T(8,128)(2,1)}, bf16[2,96,2048]{2,1,0:T(8,128)(2,1)}, u32[]{:S(2)}, u32[]{:S(2)}) collective-permute-start(bf16[2,96,2048]{2,1,0:T(8,128)(2,1)} %copy-done.4), channel_id=1, source_target_pairs={{0,4},{4,0},{8,12},{12,8},{1,5},{5,1},{9,13},{13,9},{2,6},{6,2},{1... | collective-permute-start | bytes 2359304 | tf_op jit(solution)/shard_map/ppermute | solution.py:21
  236.9 44.2 %collective-permute-start.9 = (bf16[2,96,2048]{2,1,0:T(8,128)(2,1)}, bf16[2,96,2048]{2,1,0:T(8,128)(2,1)}, u32[]{:S(2)}, u32[]{:S(2)}) collective-permute-start(bf16[2,96,2048]{2,1,0:T(8,128)(2,1)} %copy-done.32), channel_id=1, source_target_pairs={{0,4},{4,0},{8,12},{12,8},{1,5},{5,1},{9,13},{13,9},{2,6},{6,2},{1... | collective-permute-start | bytes 2359304 | tf_op jit(solution)/shard_map/ppermute | solution.py:21
  291.2 32.3 %all-to-all-start.1 = ((f32[16,8,384]{2,1,0:T(8,128)}), f32[16,8,384]{2,1,0:T(8,128)S(1)}, u32[]{:S(2)}, u32[]{:S(2)}) async-start(f32[16,8,384]{2,1,0:T(8,128)} %bitcast.8), calls=%async_computation.1 | async-start | bytes 393216 | tf_op jit(solution)/shard_map/all_to_all | solution.py:315
  350.2 18.9 %all-to-all-start.3 = ((bf16[32,29,256]{2,1,0:T(8,128)(2,1)}), bf16[32,29,256]{2,1,0:T(8,128)(2,1)S(1)}, u32[]{:S(2)}, u32[]{:S(2)}) async-start(bf16[32,29,256]{2,1,0:T(8,128)(2,1)} %get-tuple-element.24), calls=%async_computation.3 | async-start | bytes 1048576 | tf_op jit(solution)/shard_map/all_to_all | solution.py:351
  (80 other events, 1537.4 us)
